TPU v7x, 256 devices: a whole 4x4x8 slice. The times are simulated.
256 devices in a mesh: grp: 4 (over y), slab: 64 (over z, x, core).
Axes of the slice: x: 4, y: 4, z: 8, core: 2. Of those that a mesh axis runs over, the one named last changes fastest.
Arguments:
- pressure_pair: float32 [2, 1024, 256], P(None, ('grp', 'slab')), may hold values from -6 to 6
- normals: float32 [3, 1024, 256], P(None, ('grp', 'slab')), may hold values from -6 to 6
- mesh_disp: float32 [3, 1024, 128, 256], P(None, ('grp', 'slab')), may hold values from -6 to 6
- kappa: float32 [1024, 128, 256], P(('grp', 'slab')), may hold values from 1 to 10
- face_owner: int32 [262144, 1], P(('grp', 'slab')), may hold values from 0 to 63; in each aligned block of 1024 rows (0 to 1023, 1024 to 2047, ...) at most 32 rows name the same one
- face_node: int32 [262144], P(('grp', 'slab')), may hold values from 0 to 1023
- stiffness: float32 [24, 24, 262144], P(None, None, ('grp', 'slab')), may hold values from -1 to 3, as said below
- shell_conn: int32 [4, 262144], P(None, ('grp', 'slab')), may hold values from 0 to 1151
- precond: float32 [6, 262144], P(None, ('grp', 'slab')), may hold values from 0.1 to 0.3
Outputs:
- mesh_out: float32 [3, 1024, 128, 256], P(None, ('grp', 'slab'))
- shell_disp: float32 [6, 262144], P(None, ('grp', 'slab'))
Inputs may be any that keep to these rules, and one draw needn't show every extreme that they name: `face_owner`: within the 1024 faces of one device's block no owner is named by more than 32 faces, a bound that some block reaches. `stiffness`: each element's block is symmetric with diagonal entries between 2 and 3.
All inputs are finite; a program needn't handle non-finite values.
Results may differ from a plain program's by a relative error of at most 0.00011.
Values sent between devices are 32-bit elements; how exact they have to be, the bound alone decides.
No kernel may reach another device: no remote copies, remote signals or barrier semaphores. Data moves between devices by JAX's collectives and lax.ppermute only.
A program may use at most 64 MiB of HBM per device.

v0:
```python
import jax
import jax.numpy as jnp
from jax import lax
from jax.experimental import pallas as pl
from jax.experimental.pallas import tpu as pltpu
from jax.sharding import PartitionSpec as P

F32 = jnp.float32
BF16 = jnp.bfloat16
AXES = ("grp", "slab")
CAP = 32
NB = 128
NODES = 1024
EXT = NODES + NB
NBLK = EXT // 128
ELEMS = 1024
LOW = 56
VMEM = pl.BlockSpec(memory_space=pltpu.VMEM)
ANY = pl.BlockSpec(memory_space=pl.ANY)
PARAMS = pltpu.CompilerParams(vmem_limit_bytes=40 * 1024 * 1024)


def nn(a, b):
    return lax.dot_general(a, b, (((1,), (0,)), ((), ())), preferred_element_type=F32)


def nt(a, b):
    return lax.dot_general(a, b, (((1,), (1,)), ((), ())), preferred_element_type=F32)


def split(x):
    high = x.astype(BF16).astype(F32)
    return high, x - high


def iota(shape, dim):
    return lax.broadcasted_iota(jnp.int32, shape, dim)


def hot(mask):
    return jnp.where(mask, 1.0, 0.0).astype(F32)


def cat(parts, axis):
    return jnp.concatenate(parts, axis=axis)


def pack_kernel(slabs, pp, nm, own, nod, send, place):
    owners = own[...]
    nodes = nod[...].astype(F32)
    depth = pp.shape[1]

    def layer(a, z):
        return cat([a[2 * z : 2 * z + 1], a[2 * z + 1 : 2 * z + 2]], 1)

    ow = [layer(owners, z) for z in range(depth)]
    nd = [layer(nodes, z) for z in range(depth)]
    ids = iota((slabs, 256), 0)
    member = [hot(ow[z] == ids) for z in range(depth)]
    before = hot(iota((256, 256), 0) < iota((256, 256), 1)).astype(BF16)
    counts = nn(cat(member, 0).astype(BF16), before)
    offset = jnp.zeros((slabs, 1), F32)
    slot = iota((4 * CAP, 256), 0)
    rank_row = (slot // 4).astype(F32)
    comp = slot % 4
    words = []
    for z in range(depth):
        seen = counts[slabs * z : slabs * (z + 1)] + offset
        rank = jnp.sum(member[z] * seen, axis=0, keepdims=True)
        offset = offset + jnp.sum(member[z], axis=1, keepdims=True)
        place[z : z + 1] = ow[z].astype(F32) * CAP + rank
        jump = pp[0, z : z + 1] - pp[1, z : z + 1]
        t0, t1, t2 = [jump * nm[c, z : z + 1] for c in range(3)]
        value = jnp.where(comp == 0, t0, jnp.where(comp == 1, t1, jnp.where(comp == 2, t2, nd[z])))
        words.append(jnp.where(rank == rank_row, value, 0.0))
    place[depth:8] = jnp.zeros((8 - depth, 256), F32)
    high, low = split(cat(words, 1))
    members = cat(member, 1).astype(BF16)
    packed = nt(members, high.astype(BF16)) + nt(members, low.astype(BF16))
    ahead = cat([packed[1:], jnp.zeros((1, 4 * CAP), F32)], 0)
    first = send.shape[0] - 2 * slabs
    send[0:first] = jnp.zeros((first, 128), F32)
    send[pl.ds(first, slabs, stride=2), :] = packed
    send[pl.ds(first + 1, slabs, stride=2), :] = ahead


def connect(conn, table):
    c = conn[...]
    blocks = []
    for a in range(4):
        n = c[a : a + 1]
        blocks.append(n >> 7)
        table[:, a * ELEMS : (a + 1) * ELEMS] = hot(iota((128, ELEMS), 0) == (n & 127)).astype(BF16)
    return blocks


def stiff(values, blocks, stiffness, table, spread):
    high, low = split(values)
    parts = []
    for b in range(NBLK):
        lanes = slice(128 * b, 128 * b + 128)
        parts += [high[:, lanes], low[:, lanes]]
    stack = cat(parts, 0).astype(BF16)
    gathered = []
    for a in range(4):
        wide = nn(stack, table[:, a * ELEMS : (a + 1) * ELEMS])
        total = jnp.zeros((8, ELEMS), F32)
        for b in range(NBLK):
            row = wide[16 * b : 16 * b + 8] + wide[16 * b + 8 : 16 * b + 16]
            total = total + jnp.where(blocks[a] == b, row, 0.0)
        gathered.append(total)
    chunk = 256
    pieces = []
    for e in range(0, ELEMS, chunk):
        acc = jnp.zeros((24, chunk), F32)
        for a in range(4):
            for c in range(6):
                acc = acc + stiffness[a * 6 + c, :, e : e + chunk] * gathered[a][c : c + 1, e : e + chunk]
        pieces.append(acc)
    force = cat(pieces, 1)
    for a in range(4):
        part = cat([force[6 * a : 6 * a + 6], jnp.zeros((2, ELEMS), F32)], 0)
        both = cat(split(part), 0)
        for b in range(NBLK):
            spread[16 * b : 16 * b + 16, a * ELEMS : (a + 1) * ELEMS] = jnp.where(
                blocks[a] == b, both, 0.0
            ).astype(BF16)
    summed = nt(spread[...], table[...])
    return cat([summed[16 * b : 16 * b + 8] + summed[16 * b + 8 : 16 * b + 16] for b in range(NBLK)], 1)


def fold(tile):
    both = tile + pltpu.roll(tile, 4, 0)
    return jnp.where(iota(tile.shape, 0) < 3, both, 0.0)


def diagonal(precond, ghost):
    return cat([cat([precond[...], jnp.zeros((2, NODES), F32)], 0), ghost[...]], 1)


def load_kernel(recv, precond, ghost, conn, stiffness, load, first, partial, spill, edge,
                held, table, spread, slots, marks, sem):
    fetch = pltpu.make_async_copy(stiffness, held, sem)
    fetch.start()
    blocks = connect(conn, table)
    senders = recv.shape[0] // 2
    ids = iota((128, senders), 0).astype(F32)
    sums = []
    for which in range(2):
        data = recv[pl.ds(which, senders, stride=2), :].T
        high, low = split(data)
        for r in range(CAP):
            lanes = slice(r * senders, (r + 1) * senders)
            node = data[4 * r + 3 : 4 * r + 4]
            both = cat([high[4 * r : 4 * r + 4], low[4 * r : 4 * r + 4]], 0)
            if which == 0:
                block = jnp.floor(node * (1.0 / 128.0))
                node = node - 128.0 * block
                for b in range(0, 8, 2):
                    slots[8 * b : 8 * b + 16, lanes] = cat(
                        [jnp.where(block == b + k, both, 0.0) for k in range(2)], 0
                    ).astype(BF16)
            else:
                slots[0:16, lanes] = cat([both, jnp.zeros_like(both)], 0).astype(BF16)
            marks[:, lanes] = hot(ids == node).astype(BF16)
        if which == 0:
            found = nt(slots[...], marks[...])
            sums += [fold(found[8 * b : 8 * b + 8]) for b in range(8)]
        else:
            sums += [fold(nt(slots[0:16], marks[...])[0:8])]
    loading = cat(sums, 1)
    start = diagonal(precond, ghost) * loading
    load[...] = loading
    first[...] = start
    fetch.wait()
    result = stiff(start, blocks, held, table, spread)
    partial[...] = result
    spill[...] = result[:, NODES:]
    edge[...] = result[:, :NB]


def step_kernel(load, first, partial, from_low, from_high, precond, ghost, conn, stiffness, second, spill,
                held, table, spread, sem):
    fetch = pltpu.make_async_copy(stiffness, held, sem)
    fetch.start()
    blocks = connect(conn, table)
    scale = diagonal(precond, ghost)
    loading = load[...]
    extra = cat([from_low[...], jnp.zeros((8, NODES - NB), F32), from_high[...]], 1)
    values = first[...] + scale * (loading - (partial[...] + extra))
    fetch.wait()
    result = stiff(values, blocks, held, table, spread)
    own = values + scale * (loading - result)
    second[...] = own[:, :NODES]
    spill[...] = result[:, NODES:]


def reply_kernel(second, precond, from_low, recv, send, shell):
    shift = precond[:, :NB] * from_low[0:6]
    near = second[:, :NB] - cat([shift, jnp.zeros((2, NB), F32)], 0)
    values = cat([near, second[:, NB:]], 1)
    shell[...] = values[0:6]
    high, low = split(values)
    senders = recv.shape[0] // 2
    stack = cat(
        [
            part[0:4, 128 * b : 128 * b + 128]
            for b in range(NODES // 128)
            for part in (high, low)
        ],
        0,
    ).astype(BF16)
    data = recv[pl.ds(0, senders, stride=2), :].T
    ids = iota((128, senders), 0).astype(F32)
    upper = iota((8, senders), 0) < 4
    tiles = []
    for t in range(CAP // 2):
        pair = []
        for r in (2 * t, 2 * t + 1):
            node = data[4 * r + 3 : 4 * r + 4]
            block = jnp.floor(node * (1.0 / 128.0))
            wide = nn(stack, hot(ids == node - 128.0 * block).astype(BF16))
            total = jnp.zeros((8, senders), F32)
            for b in range(NODES // 128):
                total = total + jnp.where(block == b, wide[8 * b : 8 * b + 8], 0.0)
            pair.append(total + pltpu.roll(total, 4, 0))
        tiles.append(jnp.where(upper, pair[0], pair[1]))
    answer = cat(tiles, 0).T
    send[pl.ds(0, senders, stride=3), :] = cat([answer[senders - 1 :], answer[: senders - 1]], 0)
    send[pl.ds(1, senders, stride=3), :] = answer
    send[pl.ds(2, senders, stride=3), :] = cat([answer[1:], answer[:1]], 0)


def sweep_kernel(field, kappa, low_field, low_kappa, high_field, high_kappa, out, mid, factors,
                 kext, fext, mext, done, sems, out_sem):
    depth = field.shape[1]
    rows, cols = field.shape[2:]
    level = rows // 2
    flat = lax.axis_index("grp") * lax.axis_size("slab") + lax.axis_index("slab")
    last = lax.axis_size("grp") * lax.axis_size("slab") - 1
    copies = [
        pltpu.make_async_copy(src, dst, sems.at[i])
        for i, (src, dst) in enumerate(
            [
                (low_kappa, kext.at[0:2]),
                (kappa, kext.at[2 : depth + 2]),
                (high_kappa, kext.at[depth + 2 : depth + 4]),
                (low_field, fext.at[:, 0:2]),
                (field, fext.at[:, 2 : depth + 2]),
                (high_field, fext.at[:, depth + 2 : depth + 4]),
            ]
        )
    ]
    for copy in copies:
        copy.start()
    for copy in copies:
        copy.wait()

    @pl.when(flat == 0)
    def _():
        kext[1] = kext[2]

    @pl.when(flat == last)
    def _():
        kext[depth + 2] = kext[depth + 1]

    row = iota((rows, cols), 0)
    col = iota((rows, cols), 1)

    def weights(l):
        k = kext[l]
        down = k + jnp.where(row == 0, k, pltpu.roll(k, 1, 0))
        up = k + jnp.where(row == rows - 1, k, pltpu.roll(k, rows - 1, 0))
        left = k + jnp.where(col == 0, k, pltpu.roll(k, 1, 1))
        right = k + jnp.where(col == cols - 1, k, pltpu.roll(k, cols - 1, 1))
        back = k + kext[l - 1]
        front = k + kext[l + 1]
        inverse = 1.0 / (down + up + left + right + back + front)
        return (
            jnp.where(row == 0, 0.0, down) * inverse,
            jnp.where(row == rows - 1, 0.0, up) * inverse,
            jnp.where(col == 0, 0.0, left) * inverse,
            jnp.where(col == cols - 1, 0.0, right) * inverse,
            back * inverse,
            front * inverse,
        )

    def blend(w, here, before, after):
        down, up, left, right, back, front = w
        total = down * pltpu.roll(here, 1, 0) + up * pltpu.roll(here, rows - 1, 0)
        total = total + left * pltpu.roll(here, 1, 1) + right * pltpu.roll(here, cols - 1, 1)
        total = total + back * before + front * after
        return jnp.where(row == level, 0.0, total)

    fext[:, :, level : level + 1, :] = jnp.zeros((3, depth + 4, 1, cols), F32)

    def first_sweep(i, carry):
        l = i + 1
        w = weights(l)
        down, up, left, right, back, front = w
        outside = jnp.logical_or(
            jnp.logical_and(flat == 0, i == 0), jnp.logical_and(flat == last, i == depth + 1)
        )
        keep = jnp.where(outside, 0.0, 1.0)
        a, b = level - 1, level - 2
        c, d = level + 1, level + 2
        picked = [
            up[a : a + 1] * keep, back[a : a + 1], front[a : a + 1], left[a : a + 1], right[a : a + 1],
            up[b : b + 1],
            down[c : c + 1] * keep, back[c : c + 1], front[c : c + 1], left[c : c + 1], right[c : c + 1],
            down[d : d + 1],
        ]
        factors[i] = cat(picked + [jnp.zeros((4, cols), F32)], 0)
        for comp in range(3):
            mext[comp, i] = blend(w, fext[comp, l], fext[comp, l - 1], fext[comp, l + 1]) * keep
        return carry

    lax.fori_loop(0, depth + 2, first_sweep, 0)

    def second_sweep(z, carry):
        w = weights(z + 2)
        for comp in range(3):
            value = blend(w, mext[comp, z + 1], mext[comp, z], mext[comp, z + 2])
            done[comp, z] = value
            mid[comp, z] = value[LOW : LOW + 16]
        return carry

    lax.fori_loop(0, depth, second_sweep, 0)
    store = pltpu.make_async_copy(done, out, out_sem)
    store.start()
    store.wait()


def finish_kernel(slabs, recv, place, low_place, high_place, factors, mid, base, out, rows16, sem):
    depth = mid.shape[1]
    cols = mid.shape[3]
    first = recv.shape[0] - 3 * slabs
    slot = iota((4 * CAP, cols), 0)
    rank_row = (slot // 4).astype(F32)
    ids = iota((slabs, cols), 0).astype(F32)
    views = []
    for j in range(3):
        part = recv[pl.ds(first + j, slabs, stride=3), :]
        views.append(cat(split(part), 0).T.astype(BF16))
    sources = [(0, low_place[0:1])] + [(1, place[z : z + 1]) for z in range(depth)] + [(2, high_place[0:1])]
    motion = []
    for j, where in sources:
        owner = jnp.floor(where * (1.0 / CAP))
        rank = where - CAP * owner
        member = hot(owner == ids).astype(BF16)
        wide = nn(views[j], cat([member, member], 0))
        kept = jnp.where(rank == rank_row, wide, 0.0)
        total = kept[0:8]
        for t in range(1, 4 * CAP // 8):
            total = total + kept[8 * t : 8 * t + 8]
        motion.append(total + pltpu.roll(total, 4, 0))
    f = factors
    near = [[f[i, 6 * s : 6 * s + 1] * motion[i] for i in range(depth + 2)] for s in range(2)]
    for z in range(depth):
        i = z + 1
        added = []
        for s in range(2):
            o = 6 * s
            d = near[s]
            side = (
                f[i, o + 1 : o + 2] * d[i - 1]
                + f[i, o + 2 : o + 3] * d[i + 1]
                + f[i, o + 3 : o + 4] * pltpu.roll(d[i], 1, 1)
                + f[i, o + 4 : o + 5] * pltpu.roll(d[i], cols - 1, 1)
                + d[i]
            )
            added.append((side, f[i, o + 5 : o + 6] * d[i]))
        (below, below2), (above, above2) = added
        for comp in range(3):
            k = slice(comp, comp + 1)
            change = cat(
                [jnp.zeros((6, cols), F32), below2[k], below[k], motion[i][k], above[k], above2[k],
                 jnp.zeros((5, cols), F32)], 0
            )
            rows16[comp, z] = mid[comp, z] + change
    store = pltpu.make_async_copy(rows16, out.at[:, :, LOW : LOW + 16, :], sem)
    store.start()
    store.wait()


def shape(*dims):
    return jax.ShapeDtypeStruct(dims, F32)


def call(kernel, ins, outs, scratch=(), aliases=None, any_ins=(), any_outs=(), name=None):
    return pl.pallas_call(
        kernel,
        out_shape=outs,
        in_specs=[ANY if i in any_ins else VMEM for i in range(len(ins))],
        out_specs=[ANY if i in any_outs else VMEM for i in range(len(outs))],
        scratch_shapes=list(scratch),
        input_output_aliases=aliases or {},
        compiler_params=PARAMS,
        name=name,
    )(*ins)


def exchange(rows, per, count):
    flat = rows.reshape(count, 1, per * 128)
    return lax.all_to_all(flat, AXES, 0, 0, tiled=True).reshape(count * per, 128)


def on_device(
    pressure_pair, normals, mesh_disp, kappa, face_owner, face_node, stiffness, shell_conn, precond
):
    groups = lax.axis_size("grp")
    slabs = lax.axis_size("slab")
    count = groups * slabs
    depth, height, across = mesh_disp.shape[1:]
    up = [(i, i + 1) for i in range(count - 1)]
    down = [(b, a) for a, b in up]
    shell = count - slabs
    shell_up = [(shell + i, shell + i + 1) for i in range(slabs - 1)]
    shell_down = [(b, a) for a, b in shell_up]

    send, place = call(
        lambda *refs: pack_kernel(slabs, *refs),
        [pressure_pair, normals, face_owner.reshape(8, 128), face_node.reshape(8, 128)],
        [shape(2 * count, 128), shape(8, across)],
        name="pack",
    )
    ghost_own = jnp.pad(precond[:, :NB], ((0, 2), (0, 0)))
    small_down = jnp.concatenate([ghost_own, place[0:1].reshape(2, 128), jnp.zeros((6, 128), F32)], 0)
    small_up = place[depth - 1 : depth].reshape(2, 128)
    from_high = lax.ppermute(small_down, AXES, down)
    from_low = lax.ppermute(small_up, AXES, up)
    ghost = from_high[0:8]
    high_place = from_high[8:10].reshape(1, across)
    low_place = from_low.reshape(1, across)

    recv = exchange(send, 2, count)
    low_field = lax.ppermute(mesh_disp[:, depth - 2 :], AXES, up)
    high_field = lax.ppermute(mesh_disp[:, :2], AXES, down)
    low_kappa = lax.ppermute(kappa[depth - 2 :], AXES, up)
    high_kappa = lax.ppermute(kappa[:2], AXES, down)

    dense = [
        pltpu.VMEM((24, 24, ELEMS), F32),
        pltpu.VMEM((128, 4 * ELEMS), BF16),
        pltpu.VMEM((16 * NBLK, 4 * ELEMS), BF16),
    ]
    load, first, partial, spill, edge = call(
        load_kernel,
        [recv, precond, ghost, shell_conn, stiffness],
        [shape(8, EXT), shape(8, EXT), shape(8, EXT), shape(8, NB), shape(8, NB)],
        dense
        + [pltpu.VMEM((64, count * CAP), BF16), pltpu.VMEM((128, count * CAP), BF16), pltpu.SemaphoreType.DMA],
        any_ins=(4,),
        name="load",
    )
    spill_low = lax.ppermute(spill, AXES, shell_up)
    edge_high = lax.ppermute(edge, AXES, shell_down)
    second, spill = call(
        step_kernel,
        [load, first, partial, spill_low, edge_high, precond, ghost, shell_conn, stiffness],
        [shape(8, NODES), shape(8, NB)],
        dense + [pltpu.SemaphoreType.DMA],
        any_ins=(8,),
        name="step",
    )
    spill_low = lax.ppermute(spill, AXES, shell_up)
    send, shell_disp = call(
        reply_kernel,
        [second, precond, spill_low, recv],
        [shape(3 * count, 128), shape(6, NODES)],
        name="reply",
    )
    back = exchange(send, 3, count)
    base, mid, factors = call(
        sweep_kernel,
        [mesh_disp, kappa, low_field, low_kappa, high_field, high_kappa],
        [shape(3, depth, height, across), shape(3, depth, 16, across), shape(depth + 2, 16, across)],
        [
            pltpu.VMEM((depth + 4, height, across), F32),
            pltpu.VMEM((3, depth + 4, height, across), F32),
            pltpu.VMEM((3, depth + 2, height, across), F32),
            pltpu.VMEM((3, depth, height, across), F32),
            pltpu.SemaphoreType.DMA((6,)),
            pltpu.SemaphoreType.DMA,
        ],
        any_ins=range(6),
        any_outs=(0,),
        name="sweep",
    )
    (field,) = call(
        lambda *refs: finish_kernel(slabs, *refs),
        [back, place, low_place, high_place, factors, mid, base],
        [shape(3, depth, height, across)],
        [pltpu.VMEM((3, depth, 16, across), F32), pltpu.SemaphoreType.DMA],
        aliases={6: 0},
        any_ins=(6,),
        any_outs=(0,),
        name="finish",
    )
    return (field, shell_disp)


def solution(mesh):
    in_specs = (
        P(None, ("grp", "slab"), None),
        P(None, ("grp", "slab"), None),
        P(None, ("grp", "slab"), None, None),
        P(("grp", "slab"), None, None),
        P(("grp", "slab"), None),
        P(("grp", "slab")),
        P(None, None, ("grp", "slab")),
        P(None, ("grp", "slab")),
        P(None, ("grp", "slab")),
    )
    out_specs = (P(None, ("grp", "slab"), None, None), P(None, ("grp", "slab")))
    return jax.shard_map(
        on_device, mesh=mesh, in_specs=in_specs, out_specs=out_specs, check_vma=False
    )
```

profile of v0, /device:TPU:24, one launch (start us, length us, event | category | flops | bytes accessed | tf_op | source)
XLA Modules:
  0.0 104.8 jit_solution(3801981644818856275)
XLA Ops:
  0.6 0.7 copy-done.9
  1.3 0.7 copy-done.10
  2.0 0.7 copy-done.11
  2.7 0.7 copy-done.12
  3.4 1.3 %pack.1 = (f32[512,128]{1,0:T(8,128)}, f32[8,256]{1,0:T(8,128)S(1)}) custom-call(f32[2,4,256]{2,1,0:T(4,128)S(1)} %copy-done.10, f32[3,4,256]{2,1,0:T(4,128)S(1)} %copy-done.9, s32[8,128]{1,0:T(8,128)S(1)} %bitcast.15, s32[8,128]{1,0:T(8,128)S(1)} %bitcast.16), custom_call_target="tpu_custom_call" | custom-call | tf_op jit(solution)/shard_map/pack/pallas_call | solution.py:391
  4.7 14.4 %all-to-all-start = ((f32[256,1,256]{2,1,0:T(1,128)}), f32[256,1,256]{2,1,0:T(1,128)S(1)}, u32[]{:S(2)}, u32[]{:S(2)}) async-start(f32[256,1,256]{2,1,0:T(1,128)} %bitcast.2), calls=%async_computation | async-start | bytes 524288 | tf_op jit(solution)/shard_map/all_to_all | solution.py:405
  19.2 0.7 slice.27
  20.6 8.6 %collective-permute-start = (f32[16,128]{1,0:T(8,128)S(1)}, f32[16,128]{1,0:T(8,128)S(1)}, u32[]{:S(2)}, u32[]{:S(2)}) collective-permute-start(f32[16,128]{1,0:T(8,128)S(1)} %fusion), channel_id=1, source_target_pairs={{1,0},{2,1},{3,2},{4,3},{5,4},{6,5},{7,6},{8,7},{9,8},{10,9},{11,1... | collective-permute-start | bytes 24584 | tf_op jit(solution)/shard_map/ppermute | solution.py:430
  29.2 1.3 %collective-permute-done = f32[16,128]{1,0:T(8,128)S(1)} collective-permute-done((f32[16,128]{1,0:T(8,128)S(1)}, f32[16,128]{1,0:T(8,128)S(1)}, u32[]{:S(2)}, u32[]{:S(2)}) %collective-permute-start) | collective-permute-done | bytes 8224 | tf_op jit(solution)/shard_map/ppermute | solution.py:430
  30.5 2.2 %all-to-all-done = f32[256,1,256]{2,1,0:T(1,128)S(1)} async-done(((f32[256,1,256]{2,1,0:T(1,128)}), f32[256,1,256]{2,1,0:T(1,128)S(1)}, u32[]{:S(2)}, u32[]{:S(2)}) %all-to-all-start) | async-done | bytes 262176 | tf_op jit(solution)/shard_map/all_to_all | solution.py:405
  32.7 1.7 %copy-done = f32[24,24,1024]{2,1,0:T(8,128)S(1)} copy-done((f32[24,24,1024]{2,1,0:T(8,128)S(1)}, f32[24,24,1024]{2,1,0:T(8,128)}, u32[]{:S(2)}) %copy-start) | copy-done | bytes 2359320
  34.4 0.8 copy-done.5
  35.1 0.7 copy-done.8
  35.8 3.2 %load.1 = (f32[8,1152]{1,0:T(8,128)S(1)}, f32[8,1152]{1,0:T(8,128)S(1)}, f32[8,1152]{1,0:T(8,128)S(1)}, f32[8,128]{1,0:T(8,128)S(1)}, f32[8,128]{1,0:T(8,128)S(1)}) custom-call(f32[512,128]{1,0:T(8,128)S(1)} %bitcast.10, f32[6,1024]{1,0:T(8,128)S(1)} %copy-done.5, f32[8,128]{1,0:T(8,128)S(1)} %slice.36.ghost, s32[4,1024]{1,0:T(4,128)S(1)} %copy-done.8, ...), custom_call_target="tpu_custom_call" | custom-call | tf_op jit(solution)/shard_map/load/pallas_call | solution.py:391
  39.0 2.2 %collective-permute-start.1 = (f32[8,128]{1,0:T(8,128)S(1)}, f32[8,128]{1,0:T(8,128)S(1)}, u32[]{:S(2)}, u32[]{:S(2)}) collective-permute-start(f32[8,128]{1,0:T(8,128)S(1)} %get-tuple-element.21), channel_id=1, source_target_pairs={{192,193},{193,194},{194,195},{195,196},{196,197},{197,198},{198,1... | collective-permute-start | bytes 12296 | tf_op jit(solution)/shard_map/ppermute | solution.py:456
  41.3 1.3 %collective-permute-start.2 = (f32[8,128]{1,0:T(8,128)S(1)}, f32[8,128]{1,0:T(8,128)S(1)}, u32[]{:S(2)}, u32[]{:S(2)}) collective-permute-start(f32[8,128]{1,0:T(8,128)S(1)} %get-tuple-element.22), channel_id=1, source_target_pairs={{193,192},{194,193},{195,194},{196,195},{197,196},{198,197},{199,1... | collective-permute-start | bytes 12296 | tf_op jit(solution)/shard_map/ppermute | solution.py:457
  42.6 1.8 %collective-permute-done.2.from_high = f32[8,128]{1,0:T(8,128)S(1)} collective-permute-done((f32[8,128]{1,0:T(8,128)S(1)}, f32[8,128]{1,0:T(8,128)S(1)}, u32[]{:S(2)}, u32[]{:S(2)}) %collective-permute-start.2) | collective-permute-done | bytes 4128 | tf_op jit(solution)/shard_map/ppermute | solution.py:457
  44.4 1.8 %step.1 = (f32[8,1024]{1,0:T(8,128)S(1)}, f32[8,128]{1,0:T(8,128)S(1)}) custom-call(f32[8,1152]{1,0:T(8,128)S(1)} %get-tuple-element.18.load, f32[8,1152]{1,0:T(8,128)S(1)} %get-tuple-element.19.first, f32[8,1152]{1,0:T(8,128)S(1)} %get-tuple-element.20.partial, f32[8,128]{1,0:T(8,128)S(1)} %collective-permute-done.1.from_low, ...), custom_call_target="tpu_custom_call" | custom-call | tf_op jit(solution)/shard_map/step/pallas_call | solution.py:391
  46.2 4.4 %collective-permute-start.3 = (f32[8,128]{1,0:T(8,128)S(1)}, f32[8,128]{1,0:T(8,128)S(1)}, u32[]{:S(2)}, u32[]{:S(2)}) collective-permute-start(f32[8,128]{1,0:T(8,128)S(1)} %get-tuple-element.24), channel_id=1, source_target_pairs={{192,193},{193,194},{194,195},{195,196},{196,197},{197,198},{198,1... | collective-permute-start | bytes 12296 | tf_op jit(solution)/shard_map/ppermute | solution.py:466
  50.7 1.4 %fusion.1 = (f32[3,2,128,256]{3,2,1,0:T(8,128)}, f32[3,2,128,256]{3,2,1,0:T(8,128)}) fusion(f32[3,4,128,256]{3,2,1,0:T(8,128)S(1)} %copy-done.2), kind=kLoop, calls=%fused_computation.3 | loop fusion | bytes 3145728 | tf_op jit(solution)/shard_map/slice | solution.py:438
  52.0 1.9 %collective-permute-start.7 = (f32[3,2,128,256]{3,2,1,0:T(8,128)}, f32[3,2,128,256]{3,2,1,0:T(8,128)S(1)}, u32[]{:S(2)}, u32[]{:S(2)}) collective-permute-start(f32[3,2,128,256]{3,2,1,0:T(8,128)} %get-tuple-element.30), channel_id=1, source_target_pairs={{1,0},{2,1},{3,2},{4,3},{5,4},{6,5},{7,6},{8,7},{9,8},{10,9},{11,1... | collective-permute-start | bytes 2359304 | tf_op jit(solution)/shard_map/ppermute | solution.py:438
  53.9 2.4 %collective-permute-start.5 = (f32[3,2,128,256]{3,2,1,0:T(8,128)}, f32[3,2,128,256]{3,2,1,0:T(8,128)}, u32[]{:S(2)}, u32[]{:S(2)}) collective-permute-start(f32[3,2,128,256]{3,2,1,0:T(8,128)} %get-tuple-element.31), channel_id=1, source_target_pairs={{0,1},{1,2},{2,3},{3,4},{4,5},{5,6},{6,7},{7,8},{8,9},{9,10},{10,1... | collective-permute-start | bytes 2359304 | tf_op jit(solution)/shard_map/ppermute | solution.py:437
  56.4 0.8 reply.1
  57.2 0.7 copy-done.4
  57.9 16.0 %all-to-all-start.1 = ((f32[256,1,384]{2,1,0:T(1,128)}), f32[256,1,384]{2,1,0:T(1,128)S(1)}, u32[]{:S(2)}, u32[]{:S(2)}) async-start(f32[256,1,384]{2,1,0:T(1,128)} %bitcast.13), calls=%async_computation.1 | async-start | bytes 786432 | tf_op jit(solution)/shard_map/all_to_all | solution.py:405
  74.0 8.6 %collective-permute-start.8 = (f32[2,128,256]{2,1,0:T(8,128)S(1)}, f32[2,128,256]{2,1,0:T(8,128)S(1)}, u32[]{:S(2)}, u32[]{:S(2)}) collective-permute-start(f32[2,128,256]{2,1,0:T(8,128)S(1)} %get-tuple-element.32), channel_id=1, source_target_pairs={{1,0},{2,1},{3,2},{4,3},{5,4},{6,5},{7,6},{8,7},{9,8},{10,9},{11,1... | collective-permute-start | bytes 786440 | tf_op jit(solution)/shard_map/ppermute | solution.py:440
  82.6 1.9 %collective-permute-start.6 = (f32[2,128,256]{2,1,0:T(8,128)S(1)}, f32[2,128,256]{2,1,0:T(8,128)S(1)}, u32[]{:S(2)}, u32[]{:S(2)}) collective-permute-start(f32[2,128,256]{2,1,0:T(8,128)S(1)} %get-tuple-element.33), channel_id=1, source_target_pairs={{0,1},{1,2},{2,3},{3,4},{4,5},{5,6},{6,7},{7,8},{8,9},{9,10},{10,1... | collective-permute-start | bytes 786440 | tf_op jit(solution)/shard_map/ppermute | solution.py:439
  84.5 1.9 %collective-permute-start.4 = (f32[2,128]{1,0:T(2,128)}, f32[2,128]{1,0:T(2,128)S(1)}, u32[]{:S(2)}, u32[]{:S(2)}) collective-permute-start(f32[2,128]{1,0:T(2,128)} %bitcast.19), channel_id=1, source_target_pairs={{0,1},{1,2},{2,3},{3,4},{4,5},{5,6},{6,7},{7,8},{8,9},{9,10},{10,1... | collective-permute-start | bytes 3080 | tf_op jit(solution)/shard_map/ppermute | solution.py:431
  86.5 8.0 %collective-permute-done.6.low_kappa = f32[2,128,256]{2,1,0:T(8,128)S(1)} collective-permute-done((f32[2,128,256]{2,1,0:T(8,128)S(1)}, f32[2,128,256]{2,1,0:T(8,128)S(1)}, u32[]{:S(2)}, u32[]{:S(2)}) %collective-permute-start.6) | collective-permute-done | bytes 262176 | tf_op jit(solution)/shard_map/ppermute | solution.py:439
  94.5 7.7 %sweep.1 = (f32[3,4,128,256]{3,2,1,0:T(8,128)}, f32[3,4,16,256]{3,2,1,0:T(8,128)S(1)}, f32[6,16,256]{2,1,0:T(8,128)S(1)}) custom-call(f32[3,4,128,256]{3,2,1,0:T(8,128)S(1)} %copy-done.2, f32[4,128,256]{2,1,0:T(8,128)S(1)} %copy-done.3, f32[3,2,128,256]{3,2,1,0:T(8,128)} %collective-permute-done.5.low_field, ...), custom_call_target="tpu_custom_call" | custom-call | tf_op jit(solution)/shard_map/sweep/pallas_call | solution.py:391
  102.9 0.9 copy-done.7
  103.7 1.1 %finish.1 = f32[3,4,128,256]{3,2,1,0:T(8,128)} custom-call(f32[768,128]{1,0:T(8,128)S(1)} %bitcast.12, f32[8,256]{1,0:T(8,128)S(1)} %get-tuple-element.17.refs_1_, f32[1,256]{1,0:T(1,128)S(1)} %bitcast.17, f32[1,256]{1,0:T(1,128)S(1)} %bitcast.14, f32[6,16,256]{2,1,0:T(8,128)S(1)} %copy-done.7, ...), custom_call_target="tpu_custom_call", output_to_operand_aliasing={{}: (6, {})} | custom-call | tf_op jit(solution)/shard_map/finish/pallas_call | solution.py:391
  (31 shorter events, 1.4 us)
Async XLA Ops:
  0.6 0.7 copy-start.9
  1.3 0.7 copy-start.10
  2.0 0.7 copy-start.11
  2.7 0.7 copy-start.12
  4.7 27.9 %all-to-all-start = ((f32[256,1,256]{2,1,0:T(1,128)}), f32[256,1,256]{2,1,0:T(1,128)S(1)}, u32[]{:S(2)}, u32[]{:S(2)}) async-start(f32[256,1,256]{2,1,0:T(1,128)} %bitcast.2), calls=%async_computation | async-start | bytes 524288 | tf_op jit(solution)/shard_map/all_to_all | solution.py:405
  20.6 9.9 %collective-permute-start = (f32[16,128]{1,0:T(8,128)S(1)}, f32[16,128]{1,0:T(8,128)S(1)}, u32[]{:S(2)}, u32[]{:S(2)}) collective-permute-start(f32[16,128]{1,0:T(8,128)S(1)} %fusion), channel_id=1, source_target_pairs={{1,0},{2,1},{3,2},{4,3},{5,4},{6,5},{7,6},{8,7},{9,8},{10,9},{11,1... | collective-permute-start | bytes 24584 | tf_op jit(solution)/shard_map/ppermute | solution.py:430
  32.7 1.7 %copy-start = (f32[24,24,1024]{2,1,0:T(8,128)S(1)}, f32[24,24,1024]{2,1,0:T(8,128)}, u32[]{:S(2)}) copy-start(f32[24,24,1024]{2,1,0:T(8,128)} %stiffness.3) | copy-start | bytes 7077892
  34.4 0.8 copy-start.5
  35.1 0.7 copy-start.8
  35.8 8.6 %copy-start.1 = (f32[24,24,1024]{2,1,0:T(8,128)S(1)}, f32[24,24,1024]{2,1,0:T(8,128)}, u32[]{:S(2)}) copy-start(f32[24,24,1024]{2,1,0:T(8,128)} %stiffness.3) | copy-start | bytes 7077892
  39.0 11.6 %copy-start.2 = (f32[3,4,128,256]{3,2,1,0:T(8,128)S(1)}, f32[3,4,128,256]{3,2,1,0:T(8,128)}, u32[]{:S(2)}) copy-start(f32[3,4,128,256]{3,2,1,0:T(8,128)} %field.1) | copy-start | bytes 4718596
  39.0 3.6 %collective-permute-start.1 = (f32[8,128]{1,0:T(8,128)S(1)}, f32[8,128]{1,0:T(8,128)S(1)}, u32[]{:S(2)}, u32[]{:S(2)}) collective-permute-start(f32[8,128]{1,0:T(8,128)S(1)} %get-tuple-element.21), channel_id=1, source_target_pairs={{192,193},{193,194},{194,195},{195,196},{196,197},{197,198},{198,1... | collective-permute-start | bytes 12296 | tf_op jit(solution)/shard_map/ppermute | solution.py:456
  41.3 3.1 %collective-permute-start.2 = (f32[8,128]{1,0:T(8,128)S(1)}, f32[8,128]{1,0:T(8,128)S(1)}, u32[]{:S(2)}, u32[]{:S(2)}) collective-permute-start(f32[8,128]{1,0:T(8,128)S(1)} %get-tuple-element.22), channel_id=1, source_target_pairs={{193,192},{194,193},{195,194},{196,195},{197,196},{198,197},{199,1... | collective-permute-start | bytes 12296 | tf_op jit(solution)/shard_map/ppermute | solution.py:457
  46.2 27.7 %copy-start.3 = (f32[4,128,256]{2,1,0:T(8,128)S(1)}, f32[4,128,256]{2,1,0:T(8,128)}, u32[]{:S(2)}) copy-start(f32[4,128,256]{2,1,0:T(8,128)} %kappa.1) | copy-start | bytes 1572868
  46.2 10.1 %collective-permute-start.3 = (f32[8,128]{1,0:T(8,128)S(1)}, f32[8,128]{1,0:T(8,128)S(1)}, u32[]{:S(2)}, u32[]{:S(2)}) collective-permute-start(f32[8,128]{1,0:T(8,128)S(1)} %get-tuple-element.24), channel_id=1, source_target_pairs={{192,193},{193,194},{194,195},{195,196},{196,197},{197,198},{198,1... | collective-permute-start | bytes 12296 | tf_op jit(solution)/shard_map/ppermute | solution.py:466
  52.0 42.5 %collective-permute-start.7 = (f32[3,2,128,256]{3,2,1,0:T(8,128)}, f32[3,2,128,256]{3,2,1,0:T(8,128)S(1)}, u32[]{:S(2)}, u32[]{:S(2)}) collective-permute-start(f32[3,2,128,256]{3,2,1,0:T(8,128)} %get-tuple-element.30), channel_id=1, source_target_pairs={{1,0},{2,1},{3,2},{4,3},{5,4},{6,5},{7,6},{8,7},{9,8},{10,9},{11,1... | collective-permute-start | bytes 2359304 | tf_op jit(solution)/shard_map/ppermute | solution.py:438
  53.9 40.6 %collective-permute-start.5 = (f32[3,2,128,256]{3,2,1,0:T(8,128)}, f32[3,2,128,256]{3,2,1,0:T(8,128)}, u32[]{:S(2)}, u32[]{:S(2)}) collective-permute-start(f32[3,2,128,256]{3,2,1,0:T(8,128)} %get-tuple-element.31), channel_id=1, source_target_pairs={{0,1},{1,2},{2,3},{3,4},{4,5},{5,6},{6,7},{7,8},{8,9},{9,10},{10,1... | collective-permute-start | bytes 2359304 | tf_op jit(solution)/shard_map/ppermute | solution.py:437
  57.2 0.8 copy-start.4
  57.9 44.9 %all-to-all-start.1 = ((f32[256,1,384]{2,1,0:T(1,128)}), f32[256,1,384]{2,1,0:T(1,128)S(1)}, u32[]{:S(2)}, u32[]{:S(2)}) async-start(f32[256,1,384]{2,1,0:T(1,128)} %bitcast.13), calls=%async_computation.1 | async-start | bytes 786432 | tf_op jit(solution)/shard_map/all_to_all | solution.py:405
  74.0 12.5 %collective-permute-start.8 = (f32[2,128,256]{2,1,0:T(8,128)S(1)}, f32[2,128,256]{2,1,0:T(8,128)S(1)}, u32[]{:S(2)}, u32[]{:S(2)}) collective-permute-start(f32[2,128,256]{2,1,0:T(8,128)S(1)} %get-tuple-element.32), channel_id=1, source_target_pairs={{1,0},{2,1},{3,2},{4,3},{5,4},{6,5},{7,6},{8,7},{9,8},{10,9},{11,1... | collective-permute-start | bytes 786440 | tf_op jit(solution)/shard_map/ppermute | solution.py:440
  82.6 11.9 %collective-permute-start.6 = (f32[2,128,256]{2,1,0:T(8,128)S(1)}, f32[2,128,256]{2,1,0:T(8,128)S(1)}, u32[]{:S(2)}, u32[]{:S(2)}) collective-permute-start(f32[2,128,256]{2,1,0:T(8,128)S(1)} %get-tuple-element.33), channel_id=1, source_target_pairs={{0,1},{1,2},{2,3},{3,4},{4,5},{5,6},{6,7},{7,8},{8,9},{9,10},{10,1... | collective-permute-start | bytes 786440 | tf_op jit(solution)/shard_map/ppermute | solution.py:439
  84.5 18.3 %collective-permute-start.4 = (f32[2,128]{1,0:T(2,128)}, f32[2,128]{1,0:T(2,128)S(1)}, u32[]{:S(2)}, u32[]{:S(2)}) collective-permute-start(f32[2,128]{1,0:T(2,128)} %bitcast.19), channel_id=1, source_target_pairs={{0,1},{1,2},{2,3},{3,4},{4,5},{5,6},{6,7},{7,8},{8,9},{9,10},{10,1... | collective-permute-start | bytes 3080 | tf_op jit(solution)/shard_map/ppermute | solution.py:431
  102.2 0.6 copy-start.6
  102.8 0.9 copy-start.7
where the time goes:
time: 106 us; the launch traced here: 105 us
  starting transfers between devices  63.7 us (60%)
  Pallas kernels  15.9 us (15%)
  waiting for transfers between devices  13.4 us (13%)
  local copies, waits for them, and re-layouts  10.9 us (10%)
    all_to_all x2, starting transfers between devices, exchange(): lax.all_to_all(flat, AXES, 0, 0, tiled=True).reshape(count * per, 128)  30.5 us
    pallas_call x6, Pallas kernels, call(): pl.pallas_call(kernel, out_shape=outs, in_specs=[ANY if i in any_ins else...  15.9 us
    ppermute x1, starting transfers between devices, on_device(): high_kappa = lax.ppermute(kappa[:2], AXES, down)  8.58 us
    ppermute x1, starting transfers between devices, on_device(): from_high = lax.ppermute(small_down, AXES, down)  8.57 us
    unnamed x26, local copies, waits for them, and re-layouts  8.19 us
    ppermute x1, waiting for transfers between devices, on_device(): low_kappa = lax.ppermute(kappa[depth - 2:], AXES, up)  8.03 us
    ppermute x2, starting transfers between devices, on_device(): spill_low = lax.ppermute(spill, AXES, shell_up)  6.64 us
    ppermute x1, starting transfers between devices, on_device(): low_field = lax.ppermute(mesh_disp[:, depth - 2:], AXES, up)  2.41 us
  transfers between devices with their start and end apart: 11, of which 4 were waited for; matrix products, arithmetic and copies ran while one was open for 3% of the time, Pallas kernels for 8%

commit v1 on v0

--- a/solution.py
+++ b/solution.py
@@ -17,7 +17,8 @@
 LOW = 56
 VMEM = pl.BlockSpec(memory_space=pltpu.VMEM)
 ANY = pl.BlockSpec(memory_space=pl.ANY)
-PARAMS = pltpu.CompilerParams(vmem_limit_bytes=40 * 1024 * 1024)
+HBM = pl.BlockSpec(memory_space=pltpu.HBM)
+MIB = 1024 * 1024
 
 
 def nn(a, b):
@@ -45,7 +46,16 @@
     return jnp.concatenate(parts, axis=axis)
 
 
-def pack_kernel(slabs, pp, nm, own, nod, send, place):
+def fetch(sems, *pairs):
+    copies = [pltpu.make_async_copy(src, dst, sems.at[i]) for i, (src, dst) in enumerate(pairs)]
+    for copy in copies:
+        copy.start()
+    for copy in copies:
+        copy.wait()
+
+
+def pack_kernel(slabs, pp_in, nm_in, own_in, nod_in, send, place, pp, nm, own, nod, sems):
+    fetch(sems, (own_in, own), (nod_in, nod), (pp_in, pp), (nm_in, nm))
     owners = own[...]
     nodes = nod[...].astype(F32)
     depth = pp.shape[1]
@@ -84,14 +94,32 @@
     send[pl.ds(first + 1, slabs, stride=2), :] = ahead
 
 
-def connect(conn, table):
-    c = conn[...]
-    blocks = []
+def stage_kernel(field, kappa, place, stiffness, conn_in, precond_in, up, down, held, conn, precond, table, sems):
+    depth = field.shape[1]
+    rows = field.shape[2]
+    pairs = [(conn_in, conn), (precond_in, precond), (stiffness, held)]
+    for out, start in ((up, depth - 2), (down, 0)):
+        for l in range(2):
+            for c in range(3):
+                row = (2 * c + l) * rows
+                pairs.append((field.at[c, start + l], out.at[row : row + rows]))
+            row = (6 + l) * rows
+            pairs.append((kappa.at[start + l], out.at[row : row + rows]))
+    edges = place[...]
+    fill = jnp.zeros((7, edges.shape[1]), F32)
+    up[8 * rows : 8 * rows + 8] = cat([edges[depth - 1 : depth], fill], 0)
+    down[8 * rows : 8 * rows + 8] = cat([edges[0:1], fill], 0)
+    fetch(sems, *pairs)
+    connect(corners(conn), table)
+
+
+def corners(conn):
+    return [conn[a : a + 1] for a in range(4)]
+
+
+def connect(nodes, table):
     for a in range(4):
-        n = c[a : a + 1]
-        blocks.append(n >> 7)
-        table[:, a * ELEMS : (a + 1) * ELEMS] = hot(iota((128, ELEMS), 0) == (n & 127)).astype(BF16)
-    return blocks
+        table[:, a * ELEMS : (a + 1) * ELEMS] = hot(iota((128, ELEMS), 0) == (nodes[a] & 127)).astype(BF16)
 
 
 def stiff(values, blocks, stiffness, table, spread):
@@ -138,15 +166,11 @@
     return cat([cat([precond[...], jnp.zeros((2, NODES), F32)], 0), ghost[...]], 1)
 
 
-def load_kernel(recv, precond, ghost, conn, stiffness, load, first, partial, spill, edge,
-                held, table, spread, slots, marks, sem):
-    fetch = pltpu.make_async_copy(stiffness, held, sem)
-    fetch.start()
-    blocks = connect(conn, table)
+def load_kernel(recv, precond, ghost, conn, held, table, load, first, partial, spill, edge, marks, spread, slots):
+    blocks = [n >> 7 for n in corners(conn)]
     senders = recv.shape[0] // 2
     ids = iota((128, senders), 0).astype(F32)
-    sums = []
-    for which in range(2):
+    for which in (1, 0):
         data = recv[pl.ds(which, senders, stride=2), :].T
         high, low = split(data)
         for r in range(CAP):
@@ -165,37 +189,32 @@
             marks[:, lanes] = hot(ids == node).astype(BF16)
         if which == 0:
             found = nt(slots[...], marks[...])
-            sums += [fold(found[8 * b : 8 * b + 8]) for b in range(8)]
+            sums = [fold(found[8 * b : 8 * b + 8]) for b in range(8)] + sums
         else:
-            sums += [fold(nt(slots[0:16], marks[...])[0:8])]
+            sums = [fold(nt(slots[0:16], marks[...])[0:8])]
     loading = cat(sums, 1)
     start = diagonal(precond, ghost) * loading
     load[...] = loading
     first[...] = start
-    fetch.wait()
     result = stiff(start, blocks, held, table, spread)
     partial[...] = result
     spill[...] = result[:, NODES:]
     edge[...] = result[:, :NB]
 
 
-def step_kernel(load, first, partial, from_low, from_high, precond, ghost, conn, stiffness, second, spill,
-                held, table, spread, sem):
-    fetch = pltpu.make_async_copy(stiffness, held, sem)
-    fetch.start()
-    blocks = connect(conn, table)
+def step_kernel(load, first, partial, from_low, from_high, precond, ghost, conn, held, table, second, spill, spread):
+    blocks = [n >> 7 for n in corners(conn)]
     scale = diagonal(precond, ghost)
     loading = load[...]
     extra = cat([from_low[...], jnp.zeros((8, NODES - NB), F32), from_high[...]], 1)
     values = first[...] + scale * (loading - (partial[...] + extra))
-    fetch.wait()
     result = stiff(values, blocks, held, table, spread)
     own = values + scale * (loading - result)
     second[...] = own[:, :NODES]
     spill[...] = result[:, NODES:]
 
 
-def reply_kernel(second, precond, from_low, recv, send, shell):
+def reply_kernel(second, precond, from_low, recv, marks, send, shell):
     shift = precond[:, :NB] * from_low[0:6]
     near = second[:, :NB] - cat([shift, jnp.zeros((2, NB), F32)], 0)
     values = cat([near, second[:, NB:]], 1)
@@ -211,7 +230,6 @@
         0,
     ).astype(BF16)
     data = recv[pl.ds(0, senders, stride=2), :].T
-    ids = iota((128, senders), 0).astype(F32)
     upper = iota((8, senders), 0) < 4
     tiles = []
     for t in range(CAP // 2):
@@ -219,7 +237,7 @@
         for r in (2 * t, 2 * t + 1):
             node = data[4 * r + 3 : 4 * r + 4]
             block = jnp.floor(node * (1.0 / 128.0))
-            wide = nn(stack, hot(ids == node - 128.0 * block).astype(BF16))
+            wide = nn(stack, marks[:, r * senders : (r + 1) * senders])
             total = jnp.zeros((8, senders), F32)
             for b in range(NODES // 128):
                 total = total + jnp.where(block == b, wide[8 * b : 8 * b + 8], 0.0)
@@ -231,30 +249,24 @@
     send[pl.ds(2, senders, stride=3), :] = cat([answer[1:], answer[:1]], 0)
 
 
-def sweep_kernel(field, kappa, low_field, low_kappa, high_field, high_kappa, out, mid, factors,
-                 kext, fext, mext, done, sems, out_sem):
+def sweep_kernel(field, kappa, place, low, high, out, mid, factors, places,
+                 kext, fext, mext, done, edges, sems, out_sems):
     depth = field.shape[1]
     rows, cols = field.shape[2:]
     level = rows // 2
     flat = lax.axis_index("grp") * lax.axis_size("slab") + lax.axis_index("slab")
     last = lax.axis_size("grp") * lax.axis_size("slab") - 1
-    copies = [
-        pltpu.make_async_copy(src, dst, sems.at[i])
-        for i, (src, dst) in enumerate(
-            [
-                (low_kappa, kext.at[0:2]),
-                (kappa, kext.at[2 : depth + 2]),
-                (high_kappa, kext.at[depth + 2 : depth + 4]),
-                (low_field, fext.at[:, 0:2]),
-                (field, fext.at[:, 2 : depth + 2]),
-                (high_field, fext.at[:, depth + 2 : depth + 4]),
-            ]
-        )
-    ]
-    for copy in copies:
-        copy.start()
-    for copy in copies:
-        copy.wait()
+    pairs = [(kappa, kext.at[2 : depth + 2]), (field, fext.at[:, 2 : depth + 2])]
+    for side, (message, start) in enumerate(((low, 0), (high, depth + 2))):
+        pairs.append((message.at[8 * rows : 8 * rows + 8], edges.at[side]))
+        for l in range(2):
+            for c in range(3):
+                row = (2 * c + l) * rows
+                pairs.append((message.at[row : row + rows], fext.at[c, start + l]))
+            row = (6 + l) * rows
+            pairs.append((message.at[row : row + rows], kext.at[start + l]))
+    fetch(sems, *pairs)
+    places[...] = cat([edges[0, 0:1], place[0:depth], edges[1, 0:1], jnp.zeros((6 - depth, cols), F32)], 0)
 
     @pl.when(flat == 0)
     def _():
@@ -323,15 +335,17 @@
             value = blend(w, mext[comp, z + 1], mext[comp, z], mext[comp, z + 2])
             done[comp, z] = value
             mid[comp, z] = value[LOW : LOW + 16]
-        return carry
-
-    lax.fori_loop(0, depth, second_sweep, 0)
-    store = pltpu.make_async_copy(done, out, out_sem)
-    store.start()
-    store.wait()
-
-
-def finish_kernel(slabs, recv, place, low_place, high_place, factors, mid, base, out, rows16, sem):
+
+    stores = []
+    for z in range(depth):
+        second_sweep(z, 0)
+        stores.append(pltpu.make_async_copy(done.at[:, z], out.at[:, z], out_sems.at[z]))
+        stores[z].start()
+    for store in stores:
+        store.wait()
+
+
+def finish_kernel(slabs, recv, places, factors, mid, base, out, rows16, sem):
     depth = mid.shape[1]
     cols = mid.shape[3]
     first = recv.shape[0] - 3 * slabs
@@ -342,7 +356,7 @@
     for j in range(3):
         part = recv[pl.ds(first + j, slabs, stride=3), :]
         views.append(cat(split(part), 0).T.astype(BF16))
-    sources = [(0, low_place[0:1])] + [(1, place[z : z + 1]) for z in range(depth)] + [(2, high_place[0:1])]
+    sources = [(j, places[i : i + 1]) for i, j in enumerate([0] + [1] * depth + [2])]
     motion = []
     for j, where in sources:
         owner = jnp.floor(where * (1.0 / CAP))
@@ -387,15 +401,17 @@
     return jax.ShapeDtypeStruct(dims, F32)
 
 
-def call(kernel, ins, outs, scratch=(), aliases=None, any_ins=(), any_outs=(), name=None):
+def call(kernel, ins, outs, scratch, mib=8, aliases=None, name=None):
+    kinds = {"v": VMEM, "h": HBM, "a": ANY}
+    into, out = name.split("_")[1:]
     return pl.pallas_call(
         kernel,
         out_shape=outs,
-        in_specs=[ANY if i in any_ins else VMEM for i in range(len(ins))],
-        out_specs=[ANY if i in any_outs else VMEM for i in range(len(outs))],
+        in_specs=[kinds[k] for k in into],
+        out_specs=[kinds[k] for k in out],
         scratch_shapes=list(scratch),
         input_output_aliases=aliases or {},
-        compiler_params=PARAMS,
+        compiler_params=pltpu.CompilerParams(vmem_limit_bytes=mib * MIB),
         name=name,
     )(*ins)
 
@@ -417,85 +433,94 @@
     shell = count - slabs
     shell_up = [(shell + i, shell + i + 1) for i in range(slabs - 1)]
     shell_down = [(b, a) for a, b in shell_up]
+    dma = pltpu.SemaphoreType.DMA
 
     send, place = call(
         lambda *refs: pack_kernel(slabs, *refs),
         [pressure_pair, normals, face_owner.reshape(8, 128), face_node.reshape(8, 128)],
         [shape(2 * count, 128), shape(8, across)],
-        name="pack",
-    )
-    ghost_own = jnp.pad(precond[:, :NB], ((0, 2), (0, 0)))
-    small_down = jnp.concatenate([ghost_own, place[0:1].reshape(2, 128), jnp.zeros((6, 128), F32)], 0)
-    small_up = place[depth - 1 : depth].reshape(2, 128)
-    from_high = lax.ppermute(small_down, AXES, down)
-    from_low = lax.ppermute(small_up, AXES, up)
-    ghost = from_high[0:8]
-    high_place = from_high[8:10].reshape(1, across)
-    low_place = from_low.reshape(1, across)
-
+        [
+            pltpu.VMEM(pressure_pair.shape, F32),
+            pltpu.VMEM(normals.shape, F32),
+            pltpu.VMEM((8, 128), jnp.int32),
+            pltpu.VMEM((8, 128), jnp.int32),
+            dma((4,)),
+        ],
+        mib=60,
+        name="pack_hhhh_vv",
+    )
+    ghost = lax.ppermute(jnp.pad(precond[:, :NB], ((0, 2), (0, 0))), AXES, shell_down)
     recv = exchange(send, 2, count)
-    low_field = lax.ppermute(mesh_disp[:, depth - 2 :], AXES, up)
-    high_field = lax.ppermute(mesh_disp[:, :2], AXES, down)
-    low_kappa = lax.ppermute(kappa[depth - 2 :], AXES, up)
-    high_kappa = lax.ppermute(kappa[:2], AXES, down)
-
-    dense = [
-        pltpu.VMEM((24, 24, ELEMS), F32),
-        pltpu.VMEM((128, 4 * ELEMS), BF16),
-        pltpu.VMEM((16 * NBLK, 4 * ELEMS), BF16),
-    ]
-    load, first, partial, spill, edge = call(
+    message = shape(8 * height + 8, across)
+    to_up, to_down, held, conn, diag, table = call(
+        stage_kernel,
+        [mesh_disp, kappa, place, stiffness, shell_conn, precond],
+        [
+            message, message, shape(*stiffness.shape),
+            jax.ShapeDtypeStruct(shell_conn.shape, jnp.int32), shape(*precond.shape),
+            jax.ShapeDtypeStruct((128, 4 * ELEMS), BF16),
+        ],
+        [dma((19,))],
+        name="stage_hhvhhh_vvvvvv",
+    )
+    low = lax.ppermute(to_up, AXES, up)
+    high = lax.ppermute(to_down, AXES, down)
+
+    spread = pltpu.VMEM((16 * NBLK, 4 * ELEMS), BF16)
+    load, first, partial, spill, edge, marks = call(
         load_kernel,
-        [recv, precond, ghost, shell_conn, stiffness],
-        [shape(8, EXT), shape(8, EXT), shape(8, EXT), shape(8, NB), shape(8, NB)],
-        dense
-        + [pltpu.VMEM((64, count * CAP), BF16), pltpu.VMEM((128, count * CAP), BF16), pltpu.SemaphoreType.DMA],
-        any_ins=(4,),
-        name="load",
+        [recv, diag, ghost, conn, held, table],
+        [
+            shape(8, EXT), shape(8, EXT), shape(8, EXT), shape(8, NB), shape(8, NB),
+            jax.ShapeDtypeStruct((128, count * CAP), BF16),
+        ],
+        [spread, pltpu.VMEM((64, count * CAP), BF16)],
+        mib=20,
+        name="load_vvvvvv_vvvvvv",
     )
     spill_low = lax.ppermute(spill, AXES, shell_up)
     edge_high = lax.ppermute(edge, AXES, shell_down)
     second, spill = call(
         step_kernel,
-        [load, first, partial, spill_low, edge_high, precond, ghost, shell_conn, stiffness],
+        [load, first, partial, spill_low, edge_high, diag, ghost, conn, held, table],
         [shape(8, NODES), shape(8, NB)],
-        dense + [pltpu.SemaphoreType.DMA],
-        any_ins=(8,),
-        name="step",
+        [spread],
+        mib=16,
+        name="step_vvvvvvvvvv_vv",
     )
     spill_low = lax.ppermute(spill, AXES, shell_up)
     send, shell_disp = call(
         reply_kernel,
-        [second, precond, spill_low, recv],
+        [second, diag, spill_low, recv, marks],
         [shape(3 * count, 128), shape(6, NODES)],
-        name="reply",
+        [],
+        mib=12,
+        name="reply_vvvvv_vv",
     )
     back = exchange(send, 3, count)
-    base, mid, factors = call(
+    base, mid, factors, places = call(
         sweep_kernel,
-        [mesh_disp, kappa, low_field, low_kappa, high_field, high_kappa],
-        [shape(3, depth, height, across), shape(3, depth, 16, across), shape(depth + 2, 16, across)],
+        [mesh_disp, kappa, place, low, high],
+        [shape(3, depth, height, across), shape(3, depth, 16, across), shape(depth + 2, 16, across), shape(8, across)],
         [
             pltpu.VMEM((depth + 4, height, across), F32),
             pltpu.VMEM((3, depth + 4, height, across), F32),
             pltpu.VMEM((3, depth + 2, height, across), F32),
             pltpu.VMEM((3, depth, height, across), F32),
-            pltpu.SemaphoreType.DMA((6,)),
-            pltpu.SemaphoreType.DMA,
+            pltpu.VMEM((2, 8, across), F32),
+            dma((20,)),
+            dma((depth,)),
         ],
-        any_ins=range(6),
-        any_outs=(0,),
-        name="sweep",
+        mib=16,
+        name="sweep_hhvaa_hvvv",
     )
     (field,) = call(
         lambda *refs: finish_kernel(slabs, *refs),
-        [back, place, low_place, high_place, factors, mid, base],
+        [back, places, factors, mid, base],
         [shape(3, depth, height, across)],
-        [pltpu.VMEM((3, depth, 16, across), F32), pltpu.SemaphoreType.DMA],
-        aliases={6: 0},
-        any_ins=(6,),
-        any_outs=(0,),
-        name="finish",
+        [pltpu.VMEM((3, depth, 16, across), F32), dma],
+        aliases={4: 0},
+        name="finish_vvvvh_h",
     )
     return (field, shell_disp)
 

time: 106 us -> 109 us (1.028)
  the two profiles are of different devices: /device:TPU:24 before, /device:TPU:1 now
where the time goes in v1:
time: 109 us; the launch traced here: 108 us
  starting transfers between devices  67.8 us (62%)
  Pallas kernels  22.6 us (21%)
  waiting for transfers between devices  10.8 us (10%)
  local copies, waits for them, and re-layouts  6.31 us (6%)
    all_to_all x2, starting transfers between devices, exchange(): lax.all_to_all(flat, AXES, 0, 0, tiled=True).reshape(count * per, 128)  58.7 us
    pallas_call x7, Pallas kernels, call(): pl.pallas_call(kernel, out_shape=outs, in_specs=[kinds[k] for k in into],...  22.6 us
    all_to_all x2, waiting for transfers between devices, exchange(): lax.all_to_all(flat, AXES, 0, 0, tiled=True).reshape(count * per, 128)  10.8 us
    unnamed x18, local copies, waits for them, and re-layouts  6.3 us
    ppermute x1, starting transfers between devices, on_device(): low = lax.ppermute(to_up, AXES, up)  3.54 us
    ppermute x1, starting transfers between devices, on_device(): high = lax.ppermute(to_down, AXES, down)  2.88 us
  transfers between devices with their start and end apart: 8, of which 1 were waited for; matrix products, arithmetic and copies ran while one was open for 0% of the time, Pallas kernels for 18%

profile of v1, /device:TPU:1, one launch (start us, length us, event | category | flops | bytes accessed | tf_op | source)
XLA Modules:
  0.0 108.3 jit_solution(4250315730898258870)
XLA Ops:
  0.6 2.1 %pack_hhhh_vv.1 = (f32[512,128]{1,0:T(8,128)}, f32[8,256]{1,0:T(8,128)}) custom-call(f32[2,4,256]{2,1,0:T(4,128)} %refs_0_.1, f32[3,4,256]{2,1,0:T(4,128)} %refs_1_.1, s32[8,128]{1,0:T(8,128)} %bitcast.8, s32[8,128]{1,0:T(8,128)} %bitcast.9), custom_call_target="tpu_custom_call" | custom-call | tf_op jit(solution)/shard_map/pack_hhhh_vv/pallas_call | solution.py:407
  2.8 16.7 %all-to-all-start = ((f32[256,1,256]{2,1,0:T(1,128)}), f32[256,1,256]{2,1,0:T(1,128)}, u32[]{:S(2)}, u32[]{:S(2)}) async-start(f32[256,1,256]{2,1,0:T(1,128)} %bitcast.7), calls=%async_computation | async-start | bytes 524288 | tf_op jit(solution)/shard_map/all_to_all | solution.py:421
  19.4 0.0 copy-start
  19.4 1.4 %copy-done = f32[3,4,128,256]{3,2,1,0:T(8,128)S(1)} copy-done((f32[3,4,128,256]{3,2,1,0:T(8,128)S(1)}, f32[3,4,128,256]{3,2,1,0:T(8,128)}, u32[]{:S(2)}) %copy-start) | copy-done | bytes 1572888
  20.8 1.7 %copy-done.2 = f32[24,24,1024]{2,1,0:T(8,128)S(1)} copy-done((f32[24,24,1024]{2,1,0:T(8,128)S(1)}, f32[24,24,1024]{2,1,0:T(8,128)}, u32[]{:S(2)}) %copy-start.2) | copy-done | bytes 2359320
  22.5 1.0 copy-done.3
  23.5 0.8 copy-done.5
  24.3 0.7 copy-done.6
  25.0 0.7 copy-done.8
  25.7 4.4 %stage_hhvhhh_vvvvvv.1 = (f32[1032,256]{1,0:T(8,128)}, f32[1032,256]{1,0:T(8,128)}, f32[24,24,1024]{2,1,0:T(8,128)S(1)}, s32[4,1024]{1,0:T(4,128)S(1)}, f32[6,10...) custom-call(f32[3,4,128,256]{3,2,1,0:T(8,128)S(1)} %copy-done, f32[4,128,256]{2,1,0:T(8,128)S(1)} %copy-done.3, ...), custom_call_target="tpu_custom_call" | custom-call | tf_op jit(solution)/shard_map/stage_hhvhhh_vvvvvv/pallas_call | solution.py:407
  30.2 3.5 %collective-permute-start.4 = (f32[1032,256]{1,0:T(8,128)}, f32[1032,256]{1,0:T(8,128)}, u32[]{:S(2)}, u32[]{:S(2)}) collective-permute-start(f32[1032,256]{1,0:T(8,128)} %get-tuple-element.39), channel_id=1, source_target_pairs={{0,1},{1,2},{2,3},{3,4},{4,5},{5,6},{6,7},{7,8},{8,9},{9,10},{10,1... | collective-permute-start | bytes 3170312 | tf_op jit(solution)/shard_map/ppermute | solution.py:466
  33.7 2.9 %collective-permute-start.5 = (f32[1032,256]{1,0:T(8,128)}, f32[1032,256]{1,0:T(8,128)}, u32[]{:S(2)}, u32[]{:S(2)}) collective-permute-start(f32[1032,256]{1,0:T(8,128)} %get-tuple-element.40), channel_id=1, source_target_pairs={{1,0},{2,1},{3,2},{4,3},{5,4},{6,5},{7,6},{8,7},{9,8},{10,9},{11,1... | collective-permute-start | bytes 3170312 | tf_op jit(solution)/shard_map/ppermute | solution.py:467
  36.6 0.7 collective-permute-start
  37.3 0.0 collective-permute-done.ghost
  37.3 0.0 all-to-all-done
  37.3 3.7 %load_vvvvvv_vvvvvv.1 = (f32[8,1152]{1,0:T(8,128)S(1)}, f32[8,1152]{1,0:T(8,128)S(1)}, f32[8,1152]{1,0:T(8,128)S(1)}, f32[8,128]{1,0:T(8,128)S(1)}, f32[8,128]{1,0:T(8,128)S(1)}, /*index=5*/bf16[128,8192]{1,0:T(8,128)(2,1)S(1)}) custom-call(f32[512,128]{1,0:T(8,128)} %bitcast.3.recv, f32[6,1024]{1,0:T(8,128)S(1)} %get-tuple-element.26.precond, ...), custom_call_target="tpu_custom_call" | custom-call | tf_op jit(solution)/shard_map/load_vvvvvv_vvvvvv/pallas_call | solution.py:407
  41.0 0.7 collective-permute-start.1
  41.7 0.7 collective-permute-start.2
  42.4 0.0 collective-permute-done.1.from_low
  42.4 0.0 collective-permute-done.2.from_high
  42.4 1.4 %step_vvvvvvvvvv_vv.1 = (f32[8,1024]{1,0:T(8,128)S(1)}, f32[8,128]{1,0:T(8,128)S(1)}) custom-call(f32[8,1152]{1,0:T(8,128)S(1)} %get-tuple-element.30.load, f32[8,1152]{1,0:T(8,128)S(1)} %get-tuple-element.31.first, f32[8,1152]{1,0:T(8,128)S(1)} %get-tuple-element.32.partial, f32[8,128]{1,0:T(8,128)S(1)} %collective-permute-done.1.from_low, ...), custom_call_target="tpu_custom_call" | custom-call | tf_op jit(solution)/shard_map/step_vvvvvvvvvv_vv/pallas_call | solution.py:407
  43.8 0.7 collective-permute-start.3
  44.5 0.0 collective-permute-done.3.from_low
  44.5 0.0 copy-start.1
  44.5 0.0 copy-start.4
  44.5 2.5 %reply_vvvvv_vv.1 = (f32[768,128]{1,0:T(8,128)}, f32[6,1024]{1,0:T(8,128)}) custom-call(f32[8,1024]{1,0:T(8,128)S(1)} %get-tuple-element.35.second, f32[6,1024]{1,0:T(8,128)S(1)} %get-tuple-element.26.precond, f32[8,128]{1,0:T(8,128)S(1)} %collective-permute-done.3.from_low, f32[512,128]{1,0:T(8,128)} %bitcast.3.recv, ...), custom_call_target="tpu_custom_call" | custom-call | tf_op jit(solution)/shard_map/reply_vvvvv_vv/pallas_call | solution.py:407
  47.0 42.0 %all-to-all-start.1 = ((f32[256,1,384]{2,1,0:T(1,128)}), f32[256,1,384]{2,1,0:T(1,128)S(1)}, u32[]{:S(2)}, u32[]{:S(2)}) async-start(f32[256,1,384]{2,1,0:T(1,128)} %bitcast.4), calls=%async_computation.1 | async-start | bytes 786432 | tf_op jit(solution)/shard_map/all_to_all | solution.py:421
  89.1 0.0 collective-permute-done.4.low
  89.1 0.0 collective-permute-done.5.high
  89.1 7.3 %sweep_hhvaa_hvvv.1 = (f32[3,4,128,256]{3,2,1,0:T(8,128)}, f32[3,4,16,256]{3,2,1,0:T(8,128)S(1)}, f32[6,16,256]{2,1,0:T(8,128)S(1)}, f32[8,256]{1,0:T(8,128)S(1)}) custom-call(f32[3,4,128,256]{3,2,1,0:T(8,128)S(1)} %copy-done.1, f32[4,128,256]{2,1,0:T(8,128)S(1)} %copy-done.4, f32[8,256]{1,0:T(8,128)S(1)} %copy-done.7, ...), custom_call_target="tpu_custom_call" | custom-call | tf_op jit(solution)/shard_map/sweep_hhvaa_hvvv/pallas_call | solution.py:407
  96.4 10.8 %all-to-all-done.1 = f32[256,1,384]{2,1,0:T(1,128)S(1)} async-done(((f32[256,1,384]{2,1,0:T(1,128)}), f32[256,1,384]{2,1,0:T(1,128)S(1)}, u32[]{:S(2)}, u32[]{:S(2)}) %all-to-all-start.1) | async-done | bytes 393248 | tf_op jit(solution)/shard_map/all_to_all | solution.py:421
  107.2 1.1 %finish_vvvvh_h.1 = f32[3,4,128,256]{3,2,1,0:T(8,128)} custom-call(f32[768,128]{1,0:T(8,128)S(1)} %bitcast.6, f32[8,256]{1,0:T(8,128)S(1)} %get-tuple-element.41.refs_1_, f32[6,16,256]{2,1,0:T(8,128)S(1)} %get-tuple-element.42.refs_2_, f32[3,4,16,256]{3,2,1,0:T(8,128)S(1)} %get-tuple-element.43.refs_3_, ...), custom_call_target="tpu_custom_call", output_to_operand_aliasing={{}: (4, {})} | custom-call | tf_op jit(solution)/shard_map/finish_vvvvh_h/pallas_call | solution.py:407
  (12 shorter events, 0.0 us)
Async XLA Ops:
  2.8 34.6 %all-to-all-start = ((f32[256,1,256]{2,1,0:T(1,128)}), f32[256,1,256]{2,1,0:T(1,128)}, u32[]{:S(2)}, u32[]{:S(2)}) async-start(f32[256,1,256]{2,1,0:T(1,128)} %bitcast.7), calls=%async_computation | async-start | bytes 524288 | tf_op jit(solution)/shard_map/all_to_all | solution.py:421
  19.4 1.4 %copy-start = (f32[3,4,128,256]{3,2,1,0:T(8,128)S(1)}, f32[3,4,128,256]{3,2,1,0:T(8,128)}, u32[]{:S(2)}) copy-start(f32[3,4,128,256]{3,2,1,0:T(8,128)} %field.3) | copy-start | bytes 4718596
  20.8 1.7 %copy-start.2 = (f32[24,24,1024]{2,1,0:T(8,128)S(1)}, f32[24,24,1024]{2,1,0:T(8,128)}, u32[]{:S(2)}) copy-start(f32[24,24,1024]{2,1,0:T(8,128)} %stiffness.1) | copy-start | bytes 7077892
  22.5 1.0 copy-start.3
  23.5 0.8 copy-start.5
  24.3 0.7 copy-start.6
  25.0 0.7 copy-start.8
  25.7 10.9 %slice-start = ((f32[6,1024]{1,0:T(8,128)}), f32[6,128]{1,0:T(8,128)S(1)}, s32[]{:S(2)}) async-start(f32[6,1024]{1,0:T(8,128)} %precond_in.1), calls=%async_computation.2 | async-start | bytes 8192 | tf_op jit(solution)/shard_map/slice | solution.py:452
  30.2 58.9 %collective-permute-start.4 = (f32[1032,256]{1,0:T(8,128)}, f32[1032,256]{1,0:T(8,128)}, u32[]{:S(2)}, u32[]{:S(2)}) collective-permute-start(f32[1032,256]{1,0:T(8,128)} %get-tuple-element.39), channel_id=1, source_target_pairs={{0,1},{1,2},{2,3},{3,4},{4,5},{5,6},{6,7},{7,8},{8,9},{9,10},{10,1... | collective-permute-start | bytes 3170312 | tf_op jit(solution)/shard_map/ppermute | solution.py:466
  33.7 55.4 %collective-permute-start.5 = (f32[1032,256]{1,0:T(8,128)}, f32[1032,256]{1,0:T(8,128)}, u32[]{:S(2)}, u32[]{:S(2)}) collective-permute-start(f32[1032,256]{1,0:T(8,128)} %get-tuple-element.40), channel_id=1, source_target_pairs={{1,0},{2,1},{3,2},{4,3},{5,4},{6,5},{7,6},{8,7},{9,8},{10,9},{11,1... | collective-permute-start | bytes 3170312 | tf_op jit(solution)/shard_map/ppermute | solution.py:467
  36.6 0.7 collective-permute-start
  41.0 1.3 %collective-permute-start.1 = (f32[8,128]{1,0:T(8,128)S(1)}, f32[8,128]{1,0:T(8,128)S(1)}, u32[]{:S(2)}, u32[]{:S(2)}) collective-permute-start(f32[8,128]{1,0:T(8,128)S(1)} %get-tuple-element.33), channel_id=1, source_target_pairs={{192,193},{193,194},{194,195},{195,196},{196,197},{197,198},{198,1... | collective-permute-start | bytes 12296 | tf_op jit(solution)/shard_map/ppermute | solution.py:481
  41.7 0.7 collective-permute-start.2
  43.8 0.7 collective-permute-start.3
  44.5 44.6 %copy-start.1 = (f32[3,4,128,256]{3,2,1,0:T(8,128)S(1)}, f32[3,4,128,256]{3,2,1,0:T(8,128)}, u32[]{:S(2)}) copy-start(f32[3,4,128,256]{3,2,1,0:T(8,128)} %field.3) | copy-start | bytes 4718596
  44.5 44.6 %copy-start.4 = (f32[4,128,256]{2,1,0:T(8,128)S(1)}, f32[4,128,256]{2,1,0:T(8,128)}, u32[]{:S(2)}) copy-start(f32[4,128,256]{2,1,0:T(8,128)} %kappa.3) | copy-start | bytes 1572868
  44.5 44.6 %copy-start.7 = (f32[8,256]{1,0:T(8,128)S(1)}, f32[8,256]{1,0:T(8,128)}, u32[]{:S(2)}) copy-start(f32[8,256]{1,0:T(8,128)} %get-tuple-element.25.place) | copy-start | bytes 24580
  47.0 60.2 %all-to-all-start.1 = ((f32[256,1,384]{2,1,0:T(1,128)}), f32[256,1,384]{2,1,0:T(1,128)S(1)}, u32[]{:S(2)}, u32[]{:S(2)}) async-start(f32[256,1,384]{2,1,0:T(1,128)} %bitcast.4), calls=%async_computation.1 | async-start | bytes 786432 | tf_op jit(solution)/shard_map/all_to_all | solution.py:421

commit v2 on v1

--- a/solution.py
+++ b/solution.py
@@ -46,16 +46,35 @@
     return jnp.concatenate(parts, axis=axis)
 
 
-def fetch(sems, *pairs):
+def start(sems, *pairs):
     copies = [pltpu.make_async_copy(src, dst, sems.at[i]) for i, (src, dst) in enumerate(pairs)]
     for copy in copies:
         copy.start()
+    return copies
+
+
+def finish(copies):
     for copy in copies:
         copy.wait()
 
 
-def pack_kernel(slabs, pp_in, nm_in, own_in, nod_in, send, place, pp, nm, own, nod, sems):
-    fetch(sems, (own_in, own), (nod_in, nod), (pp_in, pp), (nm_in, nm))
+def fetch(sems, *pairs):
+    finish(start(sems, *pairs))
+
+
+def pack_kernel(slabs, pp_in, nm_in, own_in, nod_in, field, kappa, send, place, up, down,
+                pp, nm, own, nod, bulk, edges, sems, bulk_sems, out_sems):
+    rows = field.shape[2]
+    first_layers = (field.shape[1] - 2, 0)
+    small = start(sems, (own_in, own), (nod_in, nod), (pp_in, pp), (nm_in, nm))
+    loads = []
+    for side, z in enumerate(first_layers):
+        loads += start(
+            bulk_sems.at[side],
+            (field.at[:, pl.ds(z, 2)], bulk.at[side, 0:3]),
+            (kappa.at[pl.ds(z, 2)], bulk.at[side, 3]),
+        )
+    finish(small)
     owners = own[...]
     nodes = nod[...].astype(F32)
     depth = pp.shape[1]
@@ -84,6 +103,17 @@
         value = jnp.where(comp == 0, t0, jnp.where(comp == 1, t1, jnp.where(comp == 2, t2, nd[z])))
         words.append(jnp.where(rank == rank_row, value, 0.0))
     place[depth:8] = jnp.zeros((8 - depth, 256), F32)
+    fill = jnp.zeros((7, 256), F32)
+    edges[0] = cat([place[depth - 1 : depth], fill], 0)
+    edges[1] = cat([place[0:1], fill], 0)
+    finish(loads)
+    stores = []
+    for side, out in enumerate((up, down)):
+        stores += start(
+            out_sems.at[side],
+            *[(bulk.at[side, c, l], out.at[pl.ds((2 * c + l) * rows, rows)]) for c in range(4) for l in range(2)],
+            (edges.at[side], out.at[pl.ds(8 * rows, 8)]),
+        )
     high, low = split(cat(words, 1))
     members = cat(member, 1).astype(BF16)
     packed = nt(members, high.astype(BF16)) + nt(members, low.astype(BF16))
@@ -92,25 +122,14 @@
     send[0:first] = jnp.zeros((first, 128), F32)
     send[pl.ds(first, slabs, stride=2), :] = packed
     send[pl.ds(first + 1, slabs, stride=2), :] = ahead
-
-
-def stage_kernel(field, kappa, place, stiffness, conn_in, precond_in, up, down, held, conn, precond, table, sems):
-    depth = field.shape[1]
-    rows = field.shape[2]
-    pairs = [(conn_in, conn), (precond_in, precond), (stiffness, held)]
-    for out, start in ((up, depth - 2), (down, 0)):
-        for l in range(2):
-            for c in range(3):
-                row = (2 * c + l) * rows
-                pairs.append((field.at[c, start + l], out.at[row : row + rows]))
-            row = (6 + l) * rows
-            pairs.append((kappa.at[start + l], out.at[row : row + rows]))
-    edges = place[...]
-    fill = jnp.zeros((7, edges.shape[1]), F32)
-    up[8 * rows : 8 * rows + 8] = cat([edges[depth - 1 : depth], fill], 0)
-    down[8 * rows : 8 * rows + 8] = cat([edges[0:1], fill], 0)
-    fetch(sems, *pairs)
+    finish(stores)
+
+
+def stage_kernel(stiffness, conn_in, precond_in, held, conn, precond, table, sems):
+    copies = start(sems, (conn_in, conn), (precond_in, precond), (stiffness, held))
+    finish(copies[:1])
     connect(corners(conn), table)
+    finish(copies[1:])
 
 
 def corners(conn):
@@ -163,10 +182,11 @@
 
 
 def diagonal(precond, ghost):
-    return cat([cat([precond[...], jnp.zeros((2, NODES), F32)], 0), ghost[...]], 1)
-
-
-def load_kernel(recv, precond, ghost, conn, held, table, load, first, partial, spill, edge, marks, spread, slots):
+    joined = cat([precond[...], ghost[:, :NB]], 1)
+    return cat([joined, jnp.zeros((2, EXT), F32)], 0)
+
+
+def load_kernel(recv, precond, ghost, conn, held, table, load, first, partial, spill, edge, spread, slots, marks):
     blocks = [n >> 7 for n in corners(conn)]
     senders = recv.shape[0] // 2
     ids = iota((128, senders), 0).astype(F32)
@@ -193,10 +213,10 @@
         else:
             sums = [fold(nt(slots[0:16], marks[...])[0:8])]
     loading = cat(sums, 1)
-    start = diagonal(precond, ghost) * loading
+    values = diagonal(precond, ghost) * loading
     load[...] = loading
-    first[...] = start
-    result = stiff(start, blocks, held, table, spread)
+    first[...] = values
+    result = stiff(values, blocks, held, table, spread)
     partial[...] = result
     spill[...] = result[:, NODES:]
     edge[...] = result[:, :NB]
@@ -214,7 +234,7 @@
     spill[...] = result[:, NODES:]
 
 
-def reply_kernel(second, precond, from_low, recv, marks, send, shell):
+def reply_kernel(second, precond, from_low, recv, send, shell):
     shift = precond[:, :NB] * from_low[0:6]
     near = second[:, :NB] - cat([shift, jnp.zeros((2, NB), F32)], 0)
     values = cat([near, second[:, NB:]], 1)
@@ -230,6 +250,7 @@
         0,
     ).astype(BF16)
     data = recv[pl.ds(0, senders, stride=2), :].T
+    ids = iota((128, senders), 0).astype(F32)
     upper = iota((8, senders), 0) < 4
     tiles = []
     for t in range(CAP // 2):
@@ -237,7 +258,7 @@
         for r in (2 * t, 2 * t + 1):
             node = data[4 * r + 3 : 4 * r + 4]
             block = jnp.floor(node * (1.0 / 128.0))
-            wide = nn(stack, marks[:, r * senders : (r + 1) * senders])
+            wide = nn(stack, hot(ids == node - 128.0 * block).astype(BF16))
             total = jnp.zeros((8, senders), F32)
             for b in range(NODES // 128):
                 total = total + jnp.where(block == b, wide[8 * b : 8 * b + 8], 0.0)
@@ -435,48 +456,48 @@
     shell_down = [(b, a) for a, b in shell_up]
     dma = pltpu.SemaphoreType.DMA
 
-    send, place = call(
+    ghost = lax.ppermute(precond, AXES, shell_down)
+    message = shape(8 * height + 8, across)
+    send, place, to_up, to_down = call(
         lambda *refs: pack_kernel(slabs, *refs),
-        [pressure_pair, normals, face_owner.reshape(8, 128), face_node.reshape(8, 128)],
-        [shape(2 * count, 128), shape(8, across)],
+        [pressure_pair, normals, face_owner.reshape(8, 128), face_node.reshape(8, 128), mesh_disp, kappa],
+        [shape(2 * count, 128), shape(8, across), message, message],
         [
             pltpu.VMEM(pressure_pair.shape, F32),
             pltpu.VMEM(normals.shape, F32),
             pltpu.VMEM((8, 128), jnp.int32),
             pltpu.VMEM((8, 128), jnp.int32),
+            pltpu.VMEM((2, 4, 2, height, across), F32),
+            pltpu.VMEM((2, 8, across), F32),
             dma((4,)),
+            dma((2, 2)),
+            dma((2, 9)),
         ],
-        mib=60,
-        name="pack_hhhh_vv",
-    )
-    ghost = lax.ppermute(jnp.pad(precond[:, :NB], ((0, 2), (0, 0))), AXES, shell_down)
+        mib=63,
+        name="pack_hhhhhh_vvhh",
+    )
     recv = exchange(send, 2, count)
-    message = shape(8 * height + 8, across)
-    to_up, to_down, held, conn, diag, table = call(
+    low = lax.ppermute(to_up, AXES, up)
+    high = lax.ppermute(to_down, AXES, down)
+
+    held, conn, diag, table = call(
         stage_kernel,
-        [mesh_disp, kappa, place, stiffness, shell_conn, precond],
+        [stiffness, shell_conn, precond],
         [
-            message, message, shape(*stiffness.shape),
-            jax.ShapeDtypeStruct(shell_conn.shape, jnp.int32), shape(*precond.shape),
+            shape(*stiffness.shape), jax.ShapeDtypeStruct(shell_conn.shape, jnp.int32), shape(*precond.shape),
             jax.ShapeDtypeStruct((128, 4 * ELEMS), BF16),
         ],
-        [dma((19,))],
-        name="stage_hhvhhh_vvvvvv",
-    )
-    low = lax.ppermute(to_up, AXES, up)
-    high = lax.ppermute(to_down, AXES, down)
-
+        [dma((3,))],
+        name="stage_hhh_vvvv",
+    )
     spread = pltpu.VMEM((16 * NBLK, 4 * ELEMS), BF16)
-    load, first, partial, spill, edge, marks = call(
+    load, first, partial, spill, edge = call(
         load_kernel,
         [recv, diag, ghost, conn, held, table],
-        [
-            shape(8, EXT), shape(8, EXT), shape(8, EXT), shape(8, NB), shape(8, NB),
-            jax.ShapeDtypeStruct((128, count * CAP), BF16),
-        ],
-        [spread, pltpu.VMEM((64, count * CAP), BF16)],
+        [shape(8, EXT), shape(8, EXT), shape(8, EXT), shape(8, NB), shape(8, NB)],
+        [spread, pltpu.VMEM((64, count * CAP), BF16), pltpu.VMEM((128, count * CAP), BF16)],
         mib=20,
-        name="load_vvvvvv_vvvvvv",
+        name="load_vvvvvv_vvvvv",
     )
     spill_low = lax.ppermute(spill, AXES, shell_up)
     edge_high = lax.ppermute(edge, AXES, shell_down)
@@ -491,11 +512,11 @@
     spill_low = lax.ppermute(spill, AXES, shell_up)
     send, shell_disp = call(
         reply_kernel,
-        [second, diag, spill_low, recv, marks],
+        [second, diag, spill_low, recv],
         [shape(3 * count, 128), shape(6, NODES)],
         [],
         mib=12,
-        name="reply_vvvvv_vv",
+        name="reply_vvvv_vv",
     )
     back = exchange(send, 3, count)
     base, mid, factors, places = call(

time: 109 us -> 100 us (0.917)
  starting transfers between devices: 67.8 us -> 60.6 us
  waiting for transfers between devices: 10.8 us -> 13.8 us
  Pallas kernels: 22.6 us -> 20.2 us
  local copies, waits for them, and re-layouts: 6.31 us -> 4.12 us
    all_to_all x2, starting transfers between devices: 58.7 us -> 51.5 us  [exchange(): lax.all_to_all(flat, AXES, 0, 0, tiled=True).reshape(count * per, 128)]
    all_to_all x2, waiting for transfers between devices: 10.8 us -> 13.8 us  [exchange(): lax.all_to_all(flat, AXES, 0, 0, tiled=True).reshape(count * per, 128)]
    pallas_call x7, Pallas kernels: 22.6 us -> 20.2 us  [call(): pl.pallas_call(kernel, out_shape=outs, in_specs=[kinds[k] for k in into],...]
    unnamed x18 -> x12, local copies, waits for them, and re-layouts: 6.3 us -> 4.12 us
  transfers between devices with their start and end apart: 8 -> 8, of which waited for: 1 -> 2; matrix products, arithmetic and copies ran while one was open for 0% -> 0% of each run, Pallas kernels for 18% -> 15%
where the time goes in v2:
time: 100 us; the launch traced here: 99.5 us
  starting transfers between devices  60.6 us (61%)
  Pallas kernels  20.2 us (20%)
  waiting for transfers between devices  13.8 us (14%)
  local copies, waits for them, and re-layouts  4.12 us (4%)
    all_to_all x2, starting transfers between devices, exchange(): lax.all_to_all(flat, AXES, 0, 0, tiled=True).reshape(count * per, 128)  51.5 us
    pallas_call x7, Pallas kernels, call(): pl.pallas_call(kernel, out_shape=outs, in_specs=[kinds[k] for k in into],...  20.2 us
    all_to_all x2, waiting for transfers between devices, exchange(): lax.all_to_all(flat, AXES, 0, 0, tiled=True).reshape(count * per, 128)  13.8 us
    unnamed x12, local copies, waits for them, and re-layouts  4.12 us
    ppermute x1, starting transfers between devices, on_device(): low = lax.ppermute(to_up, AXES, up)  3.54 us
    ppermute x1, starting transfers between devices, on_device(): high = lax.ppermute(to_down, AXES, down)  2.84 us
  transfers between devices with their start and end apart: 8, of which 2 were waited for; matrix products, arithmetic and copies ran while one was open for 0% of the time, Pallas kernels for 15%

profile of v2, /device:TPU:1, one launch (start us, length us, event | category | flops | bytes accessed | tf_op | source)
XLA Modules:
  0.0 99.5 jit_solution(14772518982320301017)
XLA Ops:
  0.6 0.0 copy-start.3
  0.6 0.0 copy-start.4
  0.7 3.9 %pack_hhhhhh_vvhh.1 = (f32[512,128]{1,0:T(8,128)}, f32[8,256]{1,0:T(8,128)}, f32[1032,256]{1,0:T(8,128)}, f32[1032,256]{1,0:T(8,128)}) custom-call(f32[2,4,256]{2,1,0:T(4,128)} %refs_0_.1, f32[3,4,256]{2,1,0:T(4,128)} %refs_1_.1, s32[8,128]{1,0:T(8,128)} %bitcast.8, s32[8,128]{1,0:T(8,128)} %bitcast.9, f32[3,4,128,256]{3,2,1,0:T(8,128)} %field.1, ...), custom_call_target="tpu_custom_call" | custom-call | tf_op jit(solution)/shard_map/pack_hhhhhh_vvhh/pallas_call | solution.py:428
  4.5 16.7 %all-to-all-start = ((f32[256,1,256]{2,1,0:T(1,128)}), f32[256,1,256]{2,1,0:T(1,128)}, u32[]{:S(2)}, u32[]{:S(2)}) async-start(f32[256,1,256]{2,1,0:T(1,128)} %bitcast.7), calls=%async_computation | async-start | bytes 524288 | tf_op jit(solution)/shard_map/all_to_all | solution.py:442
  21.2 3.5 %collective-permute-start.4 = (f32[1032,256]{1,0:T(8,128)}, f32[1032,256]{1,0:T(8,128)}, u32[]{:S(2)}, u32[]{:S(2)}) collective-permute-start(f32[1032,256]{1,0:T(8,128)} %get-tuple-element.37), channel_id=1, source_target_pairs={{0,1},{1,2},{2,3},{3,4},{4,5},{5,6},{6,7},{7,8},{8,9},{9,10},{10,1... | collective-permute-start | bytes 3170312 | tf_op jit(solution)/shard_map/ppermute | solution.py:480
  24.7 2.8 %collective-permute-start.5 = (f32[1032,256]{1,0:T(8,128)}, f32[1032,256]{1,0:T(8,128)}, u32[]{:S(2)}, u32[]{:S(2)}) collective-permute-start(f32[1032,256]{1,0:T(8,128)} %get-tuple-element.38), channel_id=1, source_target_pairs={{1,0},{2,1},{3,2},{4,3},{5,4},{6,5},{7,6},{8,7},{9,8},{10,9},{11,1... | collective-permute-start | bytes 3170312 | tf_op jit(solution)/shard_map/ppermute | solution.py:481
  27.6 0.0 copy-done.3
  27.6 0.7 collective-permute-start
  28.3 0.0 copy-done.4
  28.3 0.0 copy-start.1
  28.3 1.7 %copy-done.1 = f32[24,24,1024]{2,1,0:T(8,128)S(1)} copy-done((f32[24,24,1024]{2,1,0:T(8,128)S(1)}, f32[24,24,1024]{2,1,0:T(8,128)}, u32[]{:S(2)}) %copy-start.1) | copy-done | bytes 2359320
  29.9 0.4 stage_hhh_vvvv.1
  30.4 0.0 collective-permute-done.ghost
  30.4 5.4 %all-to-all-done = f32[256,1,256]{2,1,0:T(1,128)} async-done(((f32[256,1,256]{2,1,0:T(1,128)}), f32[256,1,256]{2,1,0:T(1,128)}, u32[]{:S(2)}, u32[]{:S(2)}) %all-to-all-start) | async-done | bytes 262176 | tf_op jit(solution)/shard_map/all_to_all | solution.py:442
  35.8 3.7 %load_vvvvvv_vvvvv.1 = (f32[8,1152]{1,0:T(8,128)S(1)}, f32[8,1152]{1,0:T(8,128)S(1)}, f32[8,1152]{1,0:T(8,128)S(1)}, f32[8,128]{1,0:T(8,128)S(1)}, f32[8,128]{1,0:T(8,128)S(1)}) custom-call(f32[512,128]{1,0:T(8,128)} %bitcast.3.recv, f32[6,1024]{1,0:T(8,128)S(1)} %get-tuple-element.24.precond, f32[6,1024]{1,0:T(8,128)S(1)} %collective-permute-done.ghost, ...), custom_call_target="tpu_custom_call" | custom-call | tf_op jit(solution)/shard_map/load_vvvvvv_vvvvv/pallas_call | solution.py:428
  39.4 0.7 collective-permute-start.1
  40.1 0.7 collective-permute-start.2
  40.8 0.0 collective-permute-done.1.from_low
  40.8 0.0 collective-permute-done.2.from_high
  40.8 1.4 %step_vvvvvvvvvv_vv.1 = (f32[8,1024]{1,0:T(8,128)S(1)}, f32[8,128]{1,0:T(8,128)S(1)}) custom-call(f32[8,1152]{1,0:T(8,128)S(1)} %get-tuple-element.28.load, f32[8,1152]{1,0:T(8,128)S(1)} %get-tuple-element.29.first, f32[8,1152]{1,0:T(8,128)S(1)} %get-tuple-element.30.partial, f32[8,128]{1,0:T(8,128)S(1)} %collective-permute-done.1.from_low, ...), custom_call_target="tpu_custom_call" | custom-call | tf_op jit(solution)/shard_map/step_vvvvvvvvvv_vv/pallas_call | solution.py:428
  42.2 0.7 collective-permute-start.3
  42.9 0.0 collective-permute-done.3.from_low
  42.9 2.5 %reply_vvvv_vv.1 = (f32[768,128]{1,0:T(8,128)}, f32[6,1024]{1,0:T(8,128)}) custom-call(f32[8,1024]{1,0:T(8,128)S(1)} %get-tuple-element.33.second, f32[6,1024]{1,0:T(8,128)S(1)} %get-tuple-element.24.precond, f32[8,128]{1,0:T(8,128)S(1)} %collective-permute-done.3.from_low, f32[512,128]{1,0:T(8,128)} %bitcast.3.recv), custom_call_target="tpu_custom_call" | custom-call | tf_op jit(solution)/shard_map/reply_vvvv_vv/pallas_call | solution.py:428
  45.4 34.9 %all-to-all-start.1 = ((f32[256,1,384]{2,1,0:T(1,128)}), f32[256,1,384]{2,1,0:T(1,128)S(1)}, u32[]{:S(2)}, u32[]{:S(2)}) async-start(f32[256,1,384]{2,1,0:T(1,128)} %bitcast.4), calls=%async_computation.1 | async-start | bytes 786432 | tf_op jit(solution)/shard_map/all_to_all | solution.py:442
  80.3 0.0 collective-permute-done.4.low
  80.3 0.0 collective-permute-done.5.high
  80.3 0.0 copy-start
  80.3 1.4 %copy-done = f32[3,4,128,256]{3,2,1,0:T(8,128)S(1)} copy-done((f32[3,4,128,256]{3,2,1,0:T(8,128)S(1)}, f32[3,4,128,256]{3,2,1,0:T(8,128)}, u32[]{:S(2)}) %copy-start) | copy-done | bytes 1572888
  81.7 1.0 %copy-done.2 = f32[4,128,256]{2,1,0:T(8,128)S(1)} copy-done((f32[4,128,256]{2,1,0:T(8,128)S(1)}, f32[4,128,256]{2,1,0:T(8,128)}, u32[]{:S(2)}) %copy-start.2) | copy-done | bytes 524312
  82.8 7.3 %sweep_hhvaa_hvvv.1 = (f32[3,4,128,256]{3,2,1,0:T(8,128)}, f32[3,4,16,256]{3,2,1,0:T(8,128)S(1)}, f32[6,16,256]{2,1,0:T(8,128)S(1)}, f32[8,256]{1,0:T(8,128)S(1)}) custom-call(f32[3,4,128,256]{3,2,1,0:T(8,128)S(1)} %copy-done, f32[4,128,256]{2,1,0:T(8,128)S(1)} %copy-done.2, f32[8,256]{1,0:T(8,128)S(1)} %copy-done.5, ...), custom_call_target="tpu_custom_call" | custom-call | tf_op jit(solution)/shard_map/sweep_hhvaa_hvvv/pallas_call | solution.py:428
  90.1 8.4 %all-to-all-done.1 = f32[256,1,384]{2,1,0:T(1,128)S(1)} async-done(((f32[256,1,384]{2,1,0:T(1,128)}), f32[256,1,384]{2,1,0:T(1,128)S(1)}, u32[]{:S(2)}, u32[]{:S(2)}) %all-to-all-start.1) | async-done | bytes 393248 | tf_op jit(solution)/shard_map/all_to_all | solution.py:442
  98.4 1.1 %finish_vvvvh_h.1 = f32[3,4,128,256]{3,2,1,0:T(8,128)} custom-call(f32[768,128]{1,0:T(8,128)S(1)} %bitcast.6, f32[8,256]{1,0:T(8,128)S(1)} %get-tuple-element.39.refs_1_, f32[6,16,256]{2,1,0:T(8,128)S(1)} %get-tuple-element.40.refs_2_, f32[3,4,16,256]{3,2,1,0:T(8,128)S(1)} %get-tuple-element.41.refs_3_, ...), custom_call_target="tpu_custom_call", output_to_operand_aliasing={{}: (4, {})} | custom-call | tf_op jit(solution)/shard_map/finish_vvvvh_h/pallas_call | solution.py:428
  (3 shorter events, 0.0 us)
Async XLA Ops:
  0.6 27.0 %copy-start.3 = (f32[6,1024]{1,0:T(8,128)S(1)}, f32[6,1024]{1,0:T(8,128)}, u32[]{:S(2)}) copy-start(f32[6,1024]{1,0:T(8,128)} %precond_in.1) | copy-start | bytes 73732
  0.6 27.6 %copy-start.4 = (s32[4,1024]{1,0:T(4,128)S(1)}, s32[4,1024]{1,0:T(4,128)}, u32[]{:S(2)}) copy-start(s32[4,1024]{1,0:T(4,128)} %conn_in.1) | copy-start | bytes 49156
  4.5 31.2 %all-to-all-start = ((f32[256,1,256]{2,1,0:T(1,128)}), f32[256,1,256]{2,1,0:T(1,128)}, u32[]{:S(2)}, u32[]{:S(2)}) async-start(f32[256,1,256]{2,1,0:T(1,128)} %bitcast.7), calls=%async_computation | async-start | bytes 524288 | tf_op jit(solution)/shard_map/all_to_all | solution.py:442
  21.2 59.1 %collective-permute-start.4 = (f32[1032,256]{1,0:T(8,128)}, f32[1032,256]{1,0:T(8,128)}, u32[]{:S(2)}, u32[]{:S(2)}) collective-permute-start(f32[1032,256]{1,0:T(8,128)} %get-tuple-element.37), channel_id=1, source_target_pairs={{0,1},{1,2},{2,3},{3,4},{4,5},{5,6},{6,7},{7,8},{8,9},{9,10},{10,1... | collective-permute-start | bytes 3170312 | tf_op jit(solution)/shard_map/ppermute | solution.py:480
  24.7 55.6 %collective-permute-start.5 = (f32[1032,256]{1,0:T(8,128)}, f32[1032,256]{1,0:T(8,128)}, u32[]{:S(2)}, u32[]{:S(2)}) collective-permute-start(f32[1032,256]{1,0:T(8,128)} %get-tuple-element.38), channel_id=1, source_target_pairs={{1,0},{2,1},{3,2},{4,3},{5,4},{6,5},{7,6},{8,7},{9,8},{10,9},{11,1... | collective-permute-start | bytes 3170312 | tf_op jit(solution)/shard_map/ppermute | solution.py:481
  27.6 2.8 %collective-permute-start = (f32[6,1024]{1,0:T(8,128)S(1)}, f32[6,1024]{1,0:T(8,128)S(1)}, u32[]{:S(2)}, u32[]{:S(2)}) collective-permute-start(f32[6,1024]{1,0:T(8,128)S(1)} %copy-done.3), channel_id=1, source_target_pairs={{193,192},{194,193},{195,194},{196,195},{197,196},{198,197},{199,1... | collective-permute-start | bytes 73736 | tf_op jit(solution)/shard_map/ppermute | solution.py:459
  28.3 1.7 %copy-start.1 = (f32[24,24,1024]{2,1,0:T(8,128)S(1)}, f32[24,24,1024]{2,1,0:T(8,128)}, u32[]{:S(2)}) copy-start(f32[24,24,1024]{2,1,0:T(8,128)} %stiffness.1) | copy-start | bytes 7077892
  39.4 1.3 %collective-permute-start.1 = (f32[8,128]{1,0:T(8,128)S(1)}, f32[8,128]{1,0:T(8,128)S(1)}, u32[]{:S(2)}, u32[]{:S(2)}) collective-permute-start(f32[8,128]{1,0:T(8,128)S(1)} %get-tuple-element.31), channel_id=1, source_target_pairs={{192,193},{193,194},{194,195},{195,196},{196,197},{197,198},{198,1... | collective-permute-start | bytes 12296 | tf_op jit(solution)/shard_map/ppermute | solution.py:502
  40.1 0.7 collective-permute-start.2
  40.8 39.5 %copy-start.5 = (f32[8,256]{1,0:T(8,128)S(1)}, f32[8,256]{1,0:T(8,128)}, u32[]{:S(2)}) copy-start(f32[8,256]{1,0:T(8,128)} %get-tuple-element.36.place) | copy-start | bytes 24580
  42.2 0.7 collective-permute-start.3
  45.4 53.0 %all-to-all-start.1 = ((f32[256,1,384]{2,1,0:T(1,128)}), f32[256,1,384]{2,1,0:T(1,128)S(1)}, u32[]{:S(2)}, u32[]{:S(2)}) async-start(f32[256,1,384]{2,1,0:T(1,128)} %bitcast.4), calls=%async_computation.1 | async-start | bytes 786432 | tf_op jit(solution)/shard_map/all_to_all | solution.py:442
  80.3 1.4 %copy-start = (f32[3,4,128,256]{3,2,1,0:T(8,128)S(1)}, f32[3,4,128,256]{3,2,1,0:T(8,128)}, u32[]{:S(2)}) copy-start(f32[3,4,128,256]{3,2,1,0:T(8,128)} %field.1) | copy-start | bytes 4718596
  81.7 1.0 %copy-start.2 = (f32[4,128,256]{2,1,0:T(8,128)S(1)}, f32[4,128,256]{2,1,0:T(8,128)}, u32[]{:S(2)}) copy-start(f32[4,128,256]{2,1,0:T(8,128)} %kappa.1) | copy-start | bytes 1572868

commit v3 on v2

--- a/solution.py
+++ b/solution.py
@@ -118,10 +118,8 @@
     members = cat(member, 1).astype(BF16)
     packed = nt(members, high.astype(BF16)) + nt(members, low.astype(BF16))
     ahead = cat([packed[1:], jnp.zeros((1, 4 * CAP), F32)], 0)
-    first = send.shape[0] - 2 * slabs
-    send[0:first] = jnp.zeros((first, 128), F32)
-    send[pl.ds(first, slabs, stride=2), :] = packed
-    send[pl.ds(first + 1, slabs, stride=2), :] = ahead
+    send[pl.ds(0, slabs, stride=2), :] = packed
+    send[pl.ds(1, slabs, stride=2), :] = ahead
     finish(stores)
 
 
@@ -186,33 +184,44 @@
     return cat([joined, jnp.zeros((2, EXT), F32)], 0)
 
 
-def load_kernel(recv, precond, ghost, conn, held, table, load, first, partial, spill, edge, spread, slots, marks):
+def selection(data, r):
+    senders = data.shape[1] // 2
+    node = data[4 * r + 3 : 4 * r + 4]
+    block = jnp.floor(node * (1.0 / 128.0))
+    lane = node - 128.0 * block
+    late = iota(node.shape, 1) >= senders
+    ids = iota((128, node.shape[1]), 0).astype(F32)
+    return jnp.where(late, block + 8.0, block), hot(ids == lane).astype(BF16)
+
+
+def sum_kernel(recv, loads, data_out, low_end, high_end, slots, marks):
+    senders = recv.shape[0] // 2
+    rows = cat([recv[pl.ds(0, senders, stride=2), :], recv[pl.ds(1, senders, stride=2), :]], 0)
+    pad = jnp.zeros((6, 128), F32)
+    low_end[...] = cat([recv[2 * senders - 2 : 2 * senders], pad], 0)
+    high_end[...] = cat([recv[0:2], pad], 0)
+    data = rows.T
+    data_out[...] = data
+    high, low = split(data)
+    width = 2 * senders
+    for r in range(CAP):
+        lanes = slice(r * width, (r + 1) * width)
+        both = cat([high[4 * r : 4 * r + 4], low[4 * r : 4 * r + 4]], 0)
+        block, mark = selection(data, r)
+        for b in range(0, 10, 2):
+            pair = [jnp.where(block == b, both, 0.0), jnp.where(block == b + 1, both, 0.0) if b < 8 else jnp.zeros_like(both)]
+            slots[8 * b : 8 * b + 16, lanes] = cat(pair, 0).astype(BF16)
+        marks[:, lanes] = mark
+    found = nt(slots[...], marks[...])
+    loads[...] = cat([fold(found[8 * b : 8 * b + 8]) for b in range(NBLK)], 1)
+
+
+def load_kernel(mine, other0, other1, other2, precond, ghost, conn, held, table,
+                load, first, partial, spill, edge, spread):
     blocks = [n >> 7 for n in corners(conn)]
-    senders = recv.shape[0] // 2
-    ids = iota((128, senders), 0).astype(F32)
-    for which in (1, 0):
-        data = recv[pl.ds(which, senders, stride=2), :].T
-        high, low = split(data)
-        for r in range(CAP):
-            lanes = slice(r * senders, (r + 1) * senders)
-            node = data[4 * r + 3 : 4 * r + 4]
-            both = cat([high[4 * r : 4 * r + 4], low[4 * r : 4 * r + 4]], 0)
-            if which == 0:
-                block = jnp.floor(node * (1.0 / 128.0))
-                node = node - 128.0 * block
-                for b in range(0, 8, 2):
-                    slots[8 * b : 8 * b + 16, lanes] = cat(
-                        [jnp.where(block == b + k, both, 0.0) for k in range(2)], 0
-                    ).astype(BF16)
-            else:
-                slots[0:16, lanes] = cat([both, jnp.zeros_like(both)], 0).astype(BF16)
-            marks[:, lanes] = hot(ids == node).astype(BF16)
-        if which == 0:
-            found = nt(slots[...], marks[...])
-            sums = [fold(found[8 * b : 8 * b + 8]) for b in range(8)] + sums
-        else:
-            sums = [fold(nt(slots[0:16], marks[...])[0:8])]
-    loading = cat(sums, 1)
+    total = mine[...] + other0[...] + other1[...] + other2[...]
+    root = lax.axis_index("grp") == lax.axis_size("grp") - 1
+    loading = total * jnp.where(root, 1.0, 0.0)
     values = diagonal(precond, ghost) * loading
     load[...] = loading
     first[...] = values
@@ -230,48 +239,49 @@
     values = first[...] + scale * (loading - (partial[...] + extra))
     result = stiff(values, blocks, held, table, spread)
     own = values + scale * (loading - result)
-    second[...] = own[:, :NODES]
+    taken = scale * result
+    second[...] = cat([own[:, :NODES], -taken[:, NODES:]], 1)
     spill[...] = result[:, NODES:]
 
 
-def reply_kernel(second, precond, from_low, recv, send, shell):
-    shift = precond[:, :NB] * from_low[0:6]
-    near = second[:, :NB] - cat([shift, jnp.zeros((2, NB), F32)], 0)
-    values = cat([near, second[:, NB:]], 1)
-    shell[...] = values[0:6]
-    high, low = split(values)
-    senders = recv.shape[0] // 2
-    stack = cat(
-        [
-            part[0:4, 128 * b : 128 * b + 128]
-            for b in range(NODES // 128)
-            for part in (high, low)
-        ],
-        0,
-    ).astype(BF16)
-    data = recv[pl.ds(0, senders, stride=2), :].T
-    ids = iota((128, senders), 0).astype(F32)
-    upper = iota((8, senders), 0) < 4
+def look_up(stack, data):
+    width = data.shape[1]
+    upper = iota((8, width), 0) < 4
     tiles = []
     for t in range(CAP // 2):
         pair = []
         for r in (2 * t, 2 * t + 1):
-            node = data[4 * r + 3 : 4 * r + 4]
-            block = jnp.floor(node * (1.0 / 128.0))
-            wide = nn(stack, hot(ids == node - 128.0 * block).astype(BF16))
-            total = jnp.zeros((8, senders), F32)
-            for b in range(NODES // 128):
+            block, mark = selection(data, r)
+            wide = nn(stack, mark)
+            total = jnp.zeros((8, width), F32)
+            for b in range(NBLK):
                 total = total + jnp.where(block == b, wide[8 * b : 8 * b + 8], 0.0)
             pair.append(total + pltpu.roll(total, 4, 0))
         tiles.append(jnp.where(upper, pair[0], pair[1]))
-    answer = cat(tiles, 0).T
-    send[pl.ds(0, senders, stride=3), :] = cat([answer[senders - 1 :], answer[: senders - 1]], 0)
-    send[pl.ds(1, senders, stride=3), :] = answer
-    send[pl.ds(2, senders, stride=3), :] = cat([answer[1:], answer[:1]], 0)
-
-
-def sweep_kernel(field, kappa, place, low, high, out, mid, factors, places,
-                 kext, fext, mext, done, edges, sems, out_sems):
+    return cat(tiles, 0).T
+
+
+def reply_kernel(mine, other0, other1, other2, data, low_rows, high_rows, send):
+    values = mine[...] + other0[...] + other1[...] + other2[...]
+    high, low = split(values)
+    parts = [p[0:4, 128 * b : 128 * b + 128] for b in range(NBLK) for p in (high, low)]
+    stack = cat(parts + [jnp.zeros((8, 128), F32)], 0).astype(BF16)
+    count = data.shape[1] // 2
+    answer = look_up(stack, data[...])
+    gap = jnp.zeros((count - 2, 128), F32)
+    ends = cat([low_rows[0:1], high_rows[0:1], gap, low_rows[1:2], high_rows[1:2], gap], 0).T
+    outer = look_up(stack, ends)
+    for w in range(2):
+        part = answer[w * count : (w + 1) * count]
+        below = outer[w * count : w * count + 1]
+        above = outer[w * count + 1 : w * count + 2]
+        send[pl.ds(w, count, stride=6), :] = cat([below, part[: count - 1]], 0)
+        send[pl.ds(2 + w, count, stride=6), :] = part
+        send[pl.ds(4 + w, count, stride=6), :] = cat([part[1:], above], 0)
+
+
+def sweep_kernel(field, kappa, place, low, high, out, mid,
+                 places, kext, fext, mext, done, edges, sems, out_sems):
     depth = field.shape[1]
     rows, cols = field.shape[2:]
     level = rows // 2
@@ -287,7 +297,9 @@
             row = (6 + l) * rows
             pairs.append((message.at[row : row + rows], kext.at[start + l]))
     fetch(sems, *pairs)
-    places[...] = cat([edges[0, 0:1], place[0:depth], edges[1, 0:1], jnp.zeros((6 - depth, cols), F32)], 0)
+    places[0:1] = edges[0, 0:1]
+    places[1 : depth + 1] = place[0:depth]
+    places[depth + 1 : depth + 2] = edges[1, 0:1]
 
     @pl.when(flat == 0)
     def _():
@@ -343,41 +355,41 @@
             down[c : c + 1] * keep, back[c : c + 1], front[c : c + 1], left[c : c + 1], right[c : c + 1],
             down[d : d + 1],
         ]
-        factors[i] = cat(picked + [jnp.zeros((4, cols), F32)], 0)
+        mid[3 * depth + i] = cat(picked + [places[pl.ds(i, 1)], jnp.zeros((3, cols), F32)], 0)
         for comp in range(3):
             mext[comp, i] = blend(w, fext[comp, l], fext[comp, l - 1], fext[comp, l + 1]) * keep
         return carry
 
     lax.fori_loop(0, depth + 2, first_sweep, 0)
 
-    def second_sweep(z, carry):
+    def second_sweep(z):
         w = weights(z + 2)
         for comp in range(3):
             value = blend(w, mext[comp, z + 1], mext[comp, z], mext[comp, z + 2])
             done[comp, z] = value
-            mid[comp, z] = value[LOW : LOW + 16]
+            mid[comp * depth + z] = value[LOW : LOW + 16]
 
     stores = []
     for z in range(depth):
-        second_sweep(z, 0)
+        second_sweep(z)
         stores.append(pltpu.make_async_copy(done.at[:, z], out.at[:, z], out_sems.at[z]))
         stores[z].start()
     for store in stores:
         store.wait()
 
 
-def finish_kernel(slabs, recv, places, factors, mid, base, out, rows16, sem):
-    depth = mid.shape[1]
-    cols = mid.shape[3]
-    first = recv.shape[0] - 3 * slabs
+def finish_kernel(slabs, recv, mid, base, out, rows16, sem):
+    depth = rows16.shape[1]
+    cols = rows16.shape[3]
     slot = iota((4 * CAP, cols), 0)
     rank_row = (slot // 4).astype(F32)
     ids = iota((slabs, cols), 0).astype(F32)
     views = []
     for j in range(3):
-        part = recv[pl.ds(first + j, slabs, stride=3), :]
+        taken = recv[pl.ds(2 * j + 1, slabs, stride=6), :]
+        part = recv[pl.ds(2 * j, slabs, stride=6), :] + cat([jnp.zeros((1, 128), F32), taken[: slabs - 1]], 0)
         views.append(cat(split(part), 0).T.astype(BF16))
-    sources = [(j, places[i : i + 1]) for i, j in enumerate([0] + [1] * depth + [2])]
+    sources = [(j, mid[3 * depth + i, 12:13]) for i, j in enumerate([0] + [1] * depth + [2])]
     motion = []
     for j, where in sources:
         owner = jnp.floor(where * (1.0 / CAP))
@@ -389,7 +401,7 @@
         for t in range(1, 4 * CAP // 8):
             total = total + kept[8 * t : 8 * t + 8]
         motion.append(total + pltpu.roll(total, 4, 0))
-    f = factors
+    f = mid.at[3 * depth : 4 * depth + 2]
     near = [[f[i, 6 * s : 6 * s + 1] * motion[i] for i in range(depth + 2)] for s in range(2)]
     for z in range(depth):
         i = z + 1
@@ -412,7 +424,7 @@
                 [jnp.zeros((6, cols), F32), below2[k], below[k], motion[i][k], above[k], above2[k],
                  jnp.zeros((5, cols), F32)], 0
             )
-            rows16[comp, z] = mid[comp, z] + change
+            rows16[comp, z] = mid[comp * depth + z] + change
     store = pltpu.make_async_copy(rows16, out.at[:, :, LOW : LOW + 16, :], sem)
     store.start()
     store.wait()
@@ -433,13 +445,12 @@
         scratch_shapes=list(scratch),
         input_output_aliases=aliases or {},
         compiler_params=pltpu.CompilerParams(vmem_limit_bytes=mib * MIB),
-        name=name,
     )(*ins)
 
 
 def exchange(rows, per, count):
     flat = rows.reshape(count, 1, per * 128)
-    return lax.all_to_all(flat, AXES, 0, 0, tiled=True).reshape(count * per, 128)
+    return lax.all_to_all(flat, "slab", 0, 0, tiled=True).reshape(count * per, 128)
 
 
 def on_device(
@@ -461,7 +472,7 @@
     send, place, to_up, to_down = call(
         lambda *refs: pack_kernel(slabs, *refs),
         [pressure_pair, normals, face_owner.reshape(8, 128), face_node.reshape(8, 128), mesh_disp, kappa],
-        [shape(2 * count, 128), shape(8, across), message, message],
+        [shape(2 * slabs, 128), shape(8, across), message, message],
         [
             pltpu.VMEM(pressure_pair.shape, F32),
             pltpu.VMEM(normals.shape, F32),
@@ -476,7 +487,7 @@
         mib=63,
         name="pack_hhhhhh_vvhh",
     )
-    recv = exchange(send, 2, count)
+    recv = exchange(send, 2, slabs)
     low = lax.ppermute(to_up, AXES, up)
     high = lax.ppermute(to_down, AXES, down)
 
@@ -491,39 +502,56 @@
         name="stage_hhh_vvvv",
     )
     spread = pltpu.VMEM((16 * NBLK, 4 * ELEMS), BF16)
+    width = 2 * slabs * CAP
+    mine, kept, low_end, high_end = call(
+        sum_kernel,
+        [recv],
+        [shape(8, EXT), shape(128, 2 * slabs), shape(8, 128), shape(8, 128)],
+        [pltpu.VMEM((80, width), BF16), pltpu.VMEM((128, width), BF16)],
+        mib=12,
+        name="sum_v_vvvv",
+    )
+    root = groups - 1
+    none = jnp.zeros((8, EXT), F32)
+    others = [lax.ppermute(mine, "grp", [(g, root)]) for g in range(root)] + [none] * (4 - groups)
+    low_rows = lax.ppermute(low_end, "grp", [(g, g + 1) for g in range(root)])
+    high_rows = lax.ppermute(high_end, "grp", [(g + 1, g) for g in range(root)])
     load, first, partial, spill, edge = call(
         load_kernel,
-        [recv, diag, ghost, conn, held, table],
+        [mine, *others, diag, ghost, conn, held, table],
         [shape(8, EXT), shape(8, EXT), shape(8, EXT), shape(8, NB), shape(8, NB)],
-        [spread, pltpu.VMEM((64, count * CAP), BF16), pltpu.VMEM((128, count * CAP), BF16)],
-        mib=20,
-        name="load_vvvvvv_vvvvv",
+        [spread],
+        mib=16,
+        name="load_vvvvvvvvv_vvvvv",
     )
     spill_low = lax.ppermute(spill, AXES, shell_up)
     edge_high = lax.ppermute(edge, AXES, shell_down)
     second, spill = call(
         step_kernel,
         [load, first, partial, spill_low, edge_high, diag, ghost, conn, held, table],
-        [shape(8, NODES), shape(8, NB)],
+        [shape(8, EXT), shape(8, NB)],
         [spread],
         mib=16,
         name="step_vvvvvvvvvv_vv",
     )
-    spill_low = lax.ppermute(spill, AXES, shell_up)
-    send, shell_disp = call(
+    others = [lax.ppermute(second, "grp", [(root, g)]) for g in range(root)] + [none] * (4 - groups)
+    (send,) = call(
         reply_kernel,
-        [second, diag, spill_low, recv],
-        [shape(3 * count, 128), shape(6, NODES)],
+        [second, *others, kept, low_rows, high_rows],
+        [shape(6 * slabs, 128)],
         [],
         mib=12,
-        name="reply_vvvv_vv",
-    )
-    back = exchange(send, 3, count)
-    base, mid, factors, places = call(
+        name="reply_vvvvvvv_v",
+    )
+    back = exchange(send, 6, slabs)
+    spill_low = lax.ppermute(spill, AXES, shell_up)
+    shell_disp = second[:6, :NODES].at[:, :NB].add(-(precond[:, :NB] * spill_low[:6]))
+    base, mid = call(
         sweep_kernel,
         [mesh_disp, kappa, place, low, high],
-        [shape(3, depth, height, across), shape(3, depth, 16, across), shape(depth + 2, 16, across), shape(8, across)],
+        [shape(3, depth, height, across), shape(4 * depth + 2, 16, across)],
         [
+            pltpu.VMEM((8, across), F32),
             pltpu.VMEM((depth + 4, height, across), F32),
             pltpu.VMEM((3, depth + 4, height, across), F32),
             pltpu.VMEM((3, depth + 2, height, across), F32),
@@ -533,15 +561,15 @@
             dma((depth,)),
         ],
         mib=16,
-        name="sweep_hhvaa_hvvv",
+        name="sweep_hhvaa_hv",
     )
     (field,) = call(
         lambda *refs: finish_kernel(slabs, *refs),
-        [back, places, factors, mid, base],
+        [back, mid, base],
         [shape(3, depth, height, across)],
         [pltpu.VMEM((3, depth, 16, across), F32), dma],
-        aliases={4: 0},
-        name="finish_vvvvh_h",
+        aliases={2: 0},
+        name="finish_vvh_h",
     )
     return (field, shell_disp)
 

time: 100 us -> 93.6 us (0.936)
  starting transfers between devices: 60.6 us -> 46.1 us
  waiting for transfers between devices: 13.8 us -> 21.1 us
  other arithmetic: 0 us -> 1.29 us
    all_to_all x2, starting transfers between devices: 51.5 us -> 24 us  [exchange(): lax.all_to_all(flat, 'slab', 0, 0, tiled=True).reshape(count * per, 128)]
    ppermute x0 -> x8, starting transfers between devices: none -> 13 us  [the longest x3 7.22 us: on_device(): lax.ppermute(mine, 'grp', [(g, root)])]
    ppermute x0 -> x8, waiting for transfers between devices: none -> 11.3 us  [the longest x3 11.1 us: on_device(): lax.ppermute(second, 'grp', [(root, g)])]
    all_to_all x2, waiting for transfers between devices: 13.8 us -> 9.79 us  [exchange(): lax.all_to_all(flat, 'slab', 0, 0, tiled=True).reshape(count * per, 128)]
    pallas_call x7 -> x8, Pallas kernels: 20.2 us -> 19.4 us  [call(): pl.pallas_call(kernel, out_shape=outs, in_specs=[kinds[k] for k in into],...]
    unnamed x12 -> x18, local copies, waits for them, and re-layouts: 4.12 us -> 3.35 us
  transfers between devices with their start and end apart: 8 -> 16, of which waited for: 2 -> 4; matrix products, arithmetic and copies ran while one was open for 0% -> 1% of each run, Pallas kernels for 15% -> 16%
where the time goes in v3:
time: 93.6 us; the launch traced here: 92.3 us
  starting transfers between devices  46.1 us (49%)
  waiting for transfers between devices  21.1 us (23%)
  Pallas kernels  19.4 us (21%)
  local copies, waits for them, and re-layouts  3.36 us (4%)
  other arithmetic  1.29 us (1%)
  between operations  1.01 us (1%)
    all_to_all x2, starting transfers between devices, exchange(): lax.all_to_all(flat, 'slab', 0, 0, tiled=True).reshape(count * per, 128)  24 us
    pallas_call x8, Pallas kernels, call(): pl.pallas_call(kernel, out_shape=outs, in_specs=[kinds[k] for k in into],...  19.4 us
    ppermute x3, waiting for transfers between devices, on_device(): lax.ppermute(second, 'grp', [(root, g)])  11.1 us
    all_to_all x2, waiting for transfers between devices, exchange(): lax.all_to_all(flat, 'slab', 0, 0, tiled=True).reshape(count * per, 128)  9.79 us
    ppermute x3, starting transfers between devices, on_device(): lax.ppermute(mine, 'grp', [(g, root)])  7.22 us
    ppermute x1, starting transfers between devices, on_device(): low = lax.ppermute(to_up, AXES, up)  4.5 us
    unnamed x18, local copies, waits for them, and re-layouts  3.35 us
    ppermute x3, starting transfers between devices, on_device(): lax.ppermute(second, 'grp', [(root, g)])  2.61 us
  transfers between devices with their start and end apart: 16, of which 4 were waited for; matrix products, arithmetic and copies ran while one was open for 1% of the time, Pallas kernels for 16%

profile of v3, /device:TPU:1, one launch (start us, length us, event | category | flops | bytes accessed | tf_op | source)
XLA Modules:
  0.0 92.3 jit_solution(3376557859307711268)
XLA Ops:
  0.7 3.8 %shard_map.104 = (f32[128,128]{1,0:T(8,128)}, f32[8,256]{1,0:T(8,128)}, f32[1032,256]{1,0:T(8,128)}, f32[1032,256]{1,0:T(8,128)}) custom-call(f32[2,4,256]{2,1,0:T(4,128)} %refs_0_.1, f32[3,4,256]{2,1,0:T(4,128)} %refs_1_.1, s32[8,128]{1,0:T(8,128)} %bitcast.9, s32[8,128]{1,0:T(8,128)} %bitcast.10, f32[3,4,128,256]{3,2,1,0:T(8,128)} %field.1, ...), custom_call_target="tpu_custom_call" | custom-call | tf_op jit(solution)/shard_map/pallas_call | solution.py:440
  4.5 4.5 %collective-permute-start.11 = (f32[1032,256]{1,0:T(8,128)}, f32[1032,256]{1,0:T(8,128)S(1)}, u32[]{:S(2)}, u32[]{:S(2)}) collective-permute-start(f32[1032,256]{1,0:T(8,128)} %get-tuple-element.51), channel_id=1, source_target_pairs={{0,1},{1,2},{2,3},{3,4},{4,5},{5,6},{6,7},{7,8},{8,9},{9,10},{10,1... | collective-permute-start | bytes 3170312 | tf_op jit(solution)/shard_map/ppermute | solution.py:491
  9.0 2.0 %collective-permute-start.12 = (f32[1032,256]{1,0:T(8,128)}, f32[1032,256]{1,0:T(8,128)}, u32[]{:S(2)}, u32[]{:S(2)}) collective-permute-start(f32[1032,256]{1,0:T(8,128)} %get-tuple-element.52), channel_id=1, source_target_pairs={{1,0},{2,1},{3,2},{4,3},{5,4},{6,5},{7,6},{8,7},{9,8},{10,9},{11,1... | collective-permute-start | bytes 3170312 | tf_op jit(solution)/shard_map/ppermute | solution.py:492
  11.0 12.9 %all-to-all-start = ((f32[64,1,256]{2,1,0:T(1,128)}), f32[64,1,256]{2,1,0:T(1,128)S(1)}, u32[]{:S(2)}, u32[]{:S(2)}) async-start(f32[64,1,256]{2,1,0:T(1,128)} %bitcast.8), calls=%async_computation | async-start | bytes 131072 | tf_op jit(solution)/shard_map/all_to_all | solution.py:453
  23.9 0.7 collective-permute-start.3
  24.6 9.4 %all-to-all-done = f32[64,1,256]{2,1,0:T(1,128)S(1)} async-done(((f32[64,1,256]{2,1,0:T(1,128)}), f32[64,1,256]{2,1,0:T(1,128)S(1)}, u32[]{:S(2)}, u32[]{:S(2)}) %all-to-all-start) | async-done | bytes 65568 | tf_op jit(solution)/shard_map/all_to_all | solution.py:453
  34.0 0.9 shard_map.105
  34.9 0.7 collective-permute-start.2
  35.5 0.7 collective-permute-start.1
  36.2 5.9 %collective-permute-start = (f32[8,1152]{1,0:T(8,128)S(1)}, f32[8,1152]{1,0:T(8,128)S(1)}, u32[]{:S(2)}, u32[]{:S(2)}) collective-permute-start(f32[8,1152]{1,0:T(8,128)S(1)} %get-tuple-element.36.mine), channel_id=1, source_target_pairs={{0,192},{1,193},{2,194},{3,195},{4,196},{5,197},{6,198},{7,199},{8... | collective-permute-start | bytes 110600 | tf_op jit(solution)/shard_map/ppermute | solution.py:516
  42.1 1.7 %copy-done.1 = f32[24,24,1024]{2,1,0:T(8,128)S(1)} copy-done((f32[24,24,1024]{2,1,0:T(8,128)S(1)}, f32[24,24,1024]{2,1,0:T(8,128)}, u32[]{:S(2)}) %copy-start.1) | copy-done | bytes 2359320
  43.8 0.4 shard_map.106
  44.2 1.4 %shard_map.107 = (f32[8,1152]{1,0:T(8,128)S(1)}, f32[8,1152]{1,0:T(8,128)S(1)}, f32[8,1152]{1,0:T(8,128)S(1)}, f32[8,128]{1,0:T(8,128)S(1)}, f32[8,128]{1,0:T(8,128)S(1)}) custom-call(f32[8,1152]{1,0:T(8,128)S(1)} %get-tuple-element.36.mine, f32[8,1152]{1,0:T(8,128)S(1)} %collective-permute-done.other0, f32[8,1152]{1,0:T(8,128)S(1)} %collective-permute-done.1.other1, ...), custom_call_target="tpu_custom_call" | custom-call | tf_op jit(solution)/shard_map/pallas_call | solution.py:440
  45.7 0.7 collective-permute-start.4
  46.3 0.7 collective-permute-start.5
  47.0 1.9 %collective-permute-start.9 = (f32[8,128]{1,0:T(8,128)S(1)}, f32[8,128]{1,0:T(8,128)S(1)}, u32[]{:S(2)}, u32[]{:S(2)}) collective-permute-start(f32[8,128]{1,0:T(8,128)S(1)} %get-tuple-element.48), channel_id=1, source_target_pairs={{0,64},{64,128},{128,192},{1,65},{65,129},{129,193},{2,66},{66,130... | collective-permute-start | bytes 12296 | tf_op jit(solution)/shard_map/ppermute | solution.py:517
  48.9 1.3 %collective-permute-start.10 = (f32[8,128]{1,0:T(8,128)S(1)}, f32[8,128]{1,0:T(8,128)S(1)}, u32[]{:S(2)}, u32[]{:S(2)}) collective-permute-start(f32[8,128]{1,0:T(8,128)S(1)} %get-tuple-element.49), channel_id=1, source_target_pairs={{64,0},{128,64},{192,128},{65,1},{129,65},{193,129},{66,2},{130,66... | collective-permute-start | bytes 12296 | tf_op jit(solution)/shard_map/ppermute | solution.py:518
  50.2 1.4 %shard_map.108 = (f32[8,1152]{1,0:T(8,128)S(1)}, f32[8,128]{1,0:T(8,128)S(1)}) custom-call(f32[8,1152]{1,0:T(8,128)S(1)} %get-tuple-element.41.load, f32[8,1152]{1,0:T(8,128)S(1)} %get-tuple-element.42.first, f32[8,1152]{1,0:T(8,128)S(1)} %get-tuple-element.43.partial, f32[8,128]{1,0:T(8,128)S(1)} %collective-permute-done.4.from_low, ...), custom_call_target="tpu_custom_call" | custom-call | tf_op jit(solution)/shard_map/pallas_call | solution.py:440
  51.6 0.7 collective-permute-start.8
  52.3 0.7 collective-permute-start.7
  53.2 1.3 %collective-permute-start.6 = (f32[8,1152]{1,0:T(8,128)S(1)}, f32[8,1152]{1,0:T(8,128)S(1)}, u32[]{:S(2)}, u32[]{:S(2)}) collective-permute-start(f32[8,1152]{1,0:T(8,128)S(1)} %get-tuple-element.46.mine), channel_id=1, source_target_pairs={{192,0},{193,1},{194,2},{195,3},{196,4},{197,5},{198,6},{199,7},{2... | collective-permute-start | bytes 110600 | tf_op jit(solution)/shard_map/ppermute | solution.py:537
  54.5 11.1 %collective-permute-done.6.other0 = f32[8,1152]{1,0:T(8,128)S(1)} collective-permute-done((f32[8,1152]{1,0:T(8,128)S(1)}, f32[8,1152]{1,0:T(8,128)S(1)}, u32[]{:S(2)}, u32[]{:S(2)}) %collective-permute-start.6) | collective-permute-done | bytes 36896 | tf_op jit(solution)/shard_map/ppermute | solution.py:537
  65.6 1.6 %shard_map.109 = f32[384,128]{1,0:T(8,128)} custom-call(f32[8,1152]{1,0:T(8,128)S(1)} %get-tuple-element.46.mine, f32[8,1152]{1,0:T(8,128)S(1)} %collective-permute-done.6.other0, f32[8,1152]{1,0:T(8,128)S(1)} %collective-permute-done.7.other1, f32[8,1152]{1,0:T(8,128)S(1)} %collective-permute-done.8.other2, f32[128,128]{1,0:T(8,128)S(1)} %get-tuple-element.47.data, ...), custom_call_target="tpu_custom_call" | custom-call | tf_op jit(solution)/shard_map/pallas_call | solution.py:440
  67.2 11.1 %all-to-all-start.1 = ((f32[64,1,768]{2,1,0:T(1,128)}), f32[64,1,768]{2,1,0:T(1,128)S(1)}, u32[]{:S(2)}, u32[]{:S(2)}) async-start(f32[64,1,768]{2,1,0:T(1,128)} %bitcast.4), calls=%async_computation.1 | async-start | bytes 393216 | tf_op jit(solution)/shard_map/all_to_all | solution.py:453
  78.3 0.7 collective-permute-start.13
  78.9 0.6 compare_reduce_fusion
  79.6 0.7 fusion
  80.3 8.8 %shard_map.110 = (f32[3,4,128,256]{3,2,1,0:T(8,128)}, f32[18,16,256]{2,1,0:T(8,128)S(1)}) custom-call(f32[3,4,128,256]{3,2,1,0:T(8,128)S(1)} %copy-done, f32[4,128,256]{2,1,0:T(8,128)S(1)} %copy-done.2, f32[8,256]{1,0:T(8,128)S(1)} %copy-done.7, f32[1032,256]{1,0:T(8,128)S(1)} %collective-permute-done.11.low, f32[1032,256]{1,0:T(8,128)} %collective-permute-done.12.high), custom_call_target="tpu_custom_call" | custom-call | tf_op jit(solution)/shard_map/pallas_call | solution.py:440
  89.2 0.7 copy-done.3
  89.9 0.4 all-to-all-done.1
  90.3 1.0 %copy-done.4 = f32[18,16,256]{2,1,0:T(8,128)S(1)} copy-done((f32[18,16,256]{2,1,0:T(8,128)S(1)}, f32[18,16,256]{2,1,0:T(8,128)}, u32[]{:S(2)}) %copy-start.4) | copy-done | bytes 294936
  91.2 1.1 %shard_map.111 = f32[3,4,128,256]{3,2,1,0:T(8,128)} custom-call(f32[384,128]{1,0:T(8,128)S(1)} %bitcast.6, f32[18,16,256]{2,1,0:T(8,128)S(1)} %copy-done.4, f32[3,4,128,256]{3,2,1,0:T(8,128)} %get-tuple-element.54.refs_2_), custom_call_target="tpu_custom_call", output_to_operand_aliasing={{}: (2, {})} | custom-call | tf_op jit(solution)/shard_map/pallas_call | solution.py:440
  (29 shorter events, 0.3 us)
Async XLA Ops:
  0.6 23.3 %copy-start.5 = (f32[6,1024]{1,0:T(8,128)S(1)}, f32[6,1024]{1,0:T(8,128)}, u32[]{:S(2)}) copy-start(f32[6,1024]{1,0:T(8,128)} %precond_in.1) | copy-start | bytes 73732
  0.6 41.5 %copy-start.6 = (s32[4,1024]{1,0:T(4,128)S(1)}, s32[4,1024]{1,0:T(4,128)}, u32[]{:S(2)}) copy-start(s32[4,1024]{1,0:T(4,128)} %conn_in.1) | copy-start | bytes 49156
  4.5 75.8 %collective-permute-start.11 = (f32[1032,256]{1,0:T(8,128)}, f32[1032,256]{1,0:T(8,128)S(1)}, u32[]{:S(2)}, u32[]{:S(2)}) collective-permute-start(f32[1032,256]{1,0:T(8,128)} %get-tuple-element.51), channel_id=1, source_target_pairs={{0,1},{1,2},{2,3},{3,4},{4,5},{5,6},{6,7},{7,8},{8,9},{9,10},{10,1... | collective-permute-start | bytes 3170312 | tf_op jit(solution)/shard_map/ppermute | solution.py:491
  9.0 71.3 %collective-permute-start.12 = (f32[1032,256]{1,0:T(8,128)}, f32[1032,256]{1,0:T(8,128)}, u32[]{:S(2)}, u32[]{:S(2)}) collective-permute-start(f32[1032,256]{1,0:T(8,128)} %get-tuple-element.52), channel_id=1, source_target_pairs={{1,0},{2,1},{3,2},{4,3},{5,4},{6,5},{7,6},{8,7},{9,8},{10,9},{11,1... | collective-permute-start | bytes 3170312 | tf_op jit(solution)/shard_map/ppermute | solution.py:492
  11.0 23.0 %all-to-all-start = ((f32[64,1,256]{2,1,0:T(1,128)}), f32[64,1,256]{2,1,0:T(1,128)S(1)}, u32[]{:S(2)}, u32[]{:S(2)}) async-start(f32[64,1,256]{2,1,0:T(1,128)} %bitcast.8), calls=%async_computation | async-start | bytes 131072 | tf_op jit(solution)/shard_map/all_to_all | solution.py:453
  23.9 12.3 %collective-permute-start.3 = (f32[6,1024]{1,0:T(8,128)S(1)}, f32[6,1024]{1,0:T(8,128)S(1)}, u32[]{:S(2)}, u32[]{:S(2)}) collective-permute-start(f32[6,1024]{1,0:T(8,128)S(1)} %copy-done.5), channel_id=1, source_target_pairs={{193,192},{194,193},{195,194},{196,195},{197,196},{198,197},{199,1... | collective-permute-start | bytes 73736 | tf_op jit(solution)/shard_map/ppermute | solution.py:470
  34.9 9.3 %collective-permute-start.2 = (f32[8,1152]{1,0:T(8,128)S(1)}, f32[8,1152]{1,0:T(8,128)S(1)}, u32[]{:S(2)}, u32[]{:S(2)}) collective-permute-start(f32[8,1152]{1,0:T(8,128)S(1)} %get-tuple-element.36.mine), channel_id=1, source_target_pairs={{128,192},{129,193},{130,194},{131,195},{132,196},{133,197},{134,1... | collective-permute-start | bytes 110600 | tf_op jit(solution)/shard_map/ppermute | solution.py:516
  35.5 8.7 %collective-permute-start.1 = (f32[8,1152]{1,0:T(8,128)S(1)}, f32[8,1152]{1,0:T(8,128)S(1)}, u32[]{:S(2)}, u32[]{:S(2)}) collective-permute-start(f32[8,1152]{1,0:T(8,128)S(1)} %get-tuple-element.36.mine), channel_id=1, source_target_pairs={{64,192},{65,193},{66,194},{67,195},{68,196},{69,197},{70,198},{71... | collective-permute-start | bytes 110600 | tf_op jit(solution)/shard_map/ppermute | solution.py:516
  36.2 8.0 %collective-permute-start = (f32[8,1152]{1,0:T(8,128)S(1)}, f32[8,1152]{1,0:T(8,128)S(1)}, u32[]{:S(2)}, u32[]{:S(2)}) collective-permute-start(f32[8,1152]{1,0:T(8,128)S(1)} %get-tuple-element.36.mine), channel_id=1, source_target_pairs={{0,192},{1,193},{2,194},{3,195},{4,196},{5,197},{6,198},{7,199},{8... | collective-permute-start | bytes 110600 | tf_op jit(solution)/shard_map/ppermute | solution.py:516
  42.1 1.7 %copy-start.1 = (f32[24,24,1024]{2,1,0:T(8,128)S(1)}, f32[24,24,1024]{2,1,0:T(8,128)}, u32[]{:S(2)}) copy-start(f32[24,24,1024]{2,1,0:T(8,128)} %stiffness.1) | copy-start | bytes 7077892
  45.7 3.2 %collective-permute-start.4 = (f32[8,128]{1,0:T(8,128)S(1)}, f32[8,128]{1,0:T(8,128)S(1)}, u32[]{:S(2)}, u32[]{:S(2)}) collective-permute-start(f32[8,128]{1,0:T(8,128)S(1)} %get-tuple-element.44), channel_id=1, source_target_pairs={{192,193},{193,194},{194,195},{195,196},{196,197},{197,198},{198,1... | collective-permute-start | bytes 12296 | tf_op jit(solution)/shard_map/ppermute | solution.py:527
  46.3 3.8 %collective-permute-start.5 = (f32[8,128]{1,0:T(8,128)S(1)}, f32[8,128]{1,0:T(8,128)S(1)}, u32[]{:S(2)}, u32[]{:S(2)}) collective-permute-start(f32[8,128]{1,0:T(8,128)S(1)} %get-tuple-element.45), channel_id=1, source_target_pairs={{193,192},{194,193},{195,194},{196,195},{197,196},{198,197},{199,1... | collective-permute-start | bytes 12296 | tf_op jit(solution)/shard_map/ppermute | solution.py:528
  47.0 5.3 %collective-permute-start.9 = (f32[8,128]{1,0:T(8,128)S(1)}, f32[8,128]{1,0:T(8,128)S(1)}, u32[]{:S(2)}, u32[]{:S(2)}) collective-permute-start(f32[8,128]{1,0:T(8,128)S(1)} %get-tuple-element.48), channel_id=1, source_target_pairs={{0,64},{64,128},{128,192},{1,65},{65,129},{129,193},{2,66},{66,130... | collective-permute-start | bytes 12296 | tf_op jit(solution)/shard_map/ppermute | solution.py:517
  48.9 4.4 %collective-permute-start.10 = (f32[8,128]{1,0:T(8,128)S(1)}, f32[8,128]{1,0:T(8,128)S(1)}, u32[]{:S(2)}, u32[]{:S(2)}) collective-permute-start(f32[8,128]{1,0:T(8,128)S(1)} %get-tuple-element.49), channel_id=1, source_target_pairs={{64,0},{128,64},{192,128},{65,1},{129,65},{193,129},{66,2},{130,66... | collective-permute-start | bytes 12296 | tf_op jit(solution)/shard_map/ppermute | solution.py:518
  50.2 30.1 %copy-start = (f32[3,4,128,256]{3,2,1,0:T(8,128)S(1)}, f32[3,4,128,256]{3,2,1,0:T(8,128)}, u32[]{:S(2)}) copy-start(f32[3,4,128,256]{3,2,1,0:T(8,128)} %field.1) | copy-start | bytes 4718596
  50.2 30.1 %copy-start.2 = (f32[4,128,256]{2,1,0:T(8,128)S(1)}, f32[4,128,256]{2,1,0:T(8,128)}, u32[]{:S(2)}) copy-start(f32[4,128,256]{2,1,0:T(8,128)} %kappa.1) | copy-start | bytes 1572868
  50.2 30.1 %copy-start.7 = (f32[8,256]{1,0:T(8,128)S(1)}, f32[8,256]{1,0:T(8,128)}, u32[]{:S(2)}) copy-start(f32[8,256]{1,0:T(8,128)} %get-tuple-element.50.place) | copy-start | bytes 24580
  51.6 2.9 %collective-permute-start.8 = (f32[8,1152]{1,0:T(8,128)S(1)}, f32[8,1152]{1,0:T(8,128)S(1)}, u32[]{:S(2)}, u32[]{:S(2)}) collective-permute-start(f32[8,1152]{1,0:T(8,128)S(1)} %get-tuple-element.46.mine), channel_id=1, source_target_pairs={{192,128},{193,129},{194,130},{195,131},{196,132},{197,133},{198,1... | collective-permute-start | bytes 110600 | tf_op jit(solution)/shard_map/ppermute | solution.py:537
  52.3 2.2 %collective-permute-start.7 = (f32[8,1152]{1,0:T(8,128)S(1)}, f32[8,1152]{1,0:T(8,128)S(1)}, u32[]{:S(2)}, u32[]{:S(2)}) collective-permute-start(f32[8,1152]{1,0:T(8,128)S(1)} %get-tuple-element.46.mine), channel_id=1, source_target_pairs={{192,64},{193,65},{194,66},{195,67},{196,68},{197,69},{198,70},{19... | collective-permute-start | bytes 110600 | tf_op jit(solution)/shard_map/ppermute | solution.py:537
  53.2 12.4 %collective-permute-start.6 = (f32[8,1152]{1,0:T(8,128)S(1)}, f32[8,1152]{1,0:T(8,128)S(1)}, u32[]{:S(2)}, u32[]{:S(2)}) collective-permute-start(f32[8,1152]{1,0:T(8,128)S(1)} %get-tuple-element.46.mine), channel_id=1, source_target_pairs={{192,0},{193,1},{194,2},{195,3},{196,4},{197,5},{198,6},{199,7},{2... | collective-permute-start | bytes 110600 | tf_op jit(solution)/shard_map/ppermute | solution.py:537
  67.2 23.1 %all-to-all-start.1 = ((f32[64,1,768]{2,1,0:T(1,128)}), f32[64,1,768]{2,1,0:T(1,128)S(1)}, u32[]{:S(2)}, u32[]{:S(2)}) async-start(f32[64,1,768]{2,1,0:T(1,128)} %bitcast.4), calls=%async_computation.1 | async-start | bytes 393216 | tf_op jit(solution)/shard_map/all_to_all | solution.py:453
  78.3 1.3 %collective-permute-start.13 = (f32[8,128]{1,0:T(8,128)S(1)}, f32[8,128]{1,0:T(8,128)S(1)}, u32[]{:S(2)}, u32[]{:S(2)}) collective-permute-start(f32[8,128]{1,0:T(8,128)S(1)} %get-tuple-element.55), channel_id=1, source_target_pairs={{192,193},{193,194},{194,195},{195,196},{196,197},{197,198},{198,1... | collective-permute-start | bytes 12296 | tf_op jit(solution)/shard_map/ppermute | solution.py:547
  80.2 8.9 %copy-start.8 = (f32[6,1024]{1,0:T(8,128)}, f32[6,1024]{1,0:T(8,128)S(1)}, u32[]{:S(2)}) copy-start(f32[6,1024]{1,0:T(8,128)S(1)} %fusion) | copy-start | bytes 73732
  89.2 0.7 copy-start.3
  90.3 1.0 %copy-start.4 = (f32[18,16,256]{2,1,0:T(8,128)S(1)}, f32[18,16,256]{2,1,0:T(8,128)}, u32[]{:S(2)}) copy-start(f32[18,16,256]{2,1,0:T(8,128)} %copy-done.3) | copy-start | bytes 884740

commit v4 on v3

--- a/solution.py
+++ b/solution.py
@@ -56,10 +56,6 @@
 def finish(copies):
     for copy in copies:
         copy.wait()
-
-
-def fetch(sems, *pairs):
-    finish(start(sems, *pairs))
 
 
 def pack_kernel(slabs, pp_in, nm_in, own_in, nod_in, field, kappa, send, place, up, down,
@@ -261,7 +257,9 @@
     return cat(tiles, 0).T
 
 
-def reply_kernel(mine, other0, other1, other2, data, low_rows, high_rows, send):
+def reply_kernel(mine, other0, other1, other2, data, low_rows, high_rows, precond, from_low, swept, send, shell):
+    shift = precond[:, :NB] * from_low[0:6]
+    shell[...] = cat([mine[0:6, :NB] - shift, mine[0:6, NB:NODES]], 1)
     values = mine[...] + other0[...] + other1[...] + other2[...]
     high, low = split(values)
     parts = [p[0:4, 128 * b : 128 * b + 128] for b in range(NBLK) for p in (high, low)]
@@ -288,26 +286,17 @@
     flat = lax.axis_index("grp") * lax.axis_size("slab") + lax.axis_index("slab")
     last = lax.axis_size("grp") * lax.axis_size("slab") - 1
     pairs = [(kappa, kext.at[2 : depth + 2]), (field, fext.at[:, 2 : depth + 2])]
-    for side, (message, start) in enumerate(((low, 0), (high, depth + 2))):
+    for side, (message, base) in enumerate(((low, 0), (high, depth + 2))):
         pairs.append((message.at[8 * rows : 8 * rows + 8], edges.at[side]))
         for l in range(2):
             for c in range(3):
                 row = (2 * c + l) * rows
-                pairs.append((message.at[row : row + rows], fext.at[c, start + l]))
+                pairs.append((message.at[row : row + rows], fext.at[c, base + l]))
             row = (6 + l) * rows
-            pairs.append((message.at[row : row + rows], kext.at[start + l]))
-    fetch(sems, *pairs)
-    places[0:1] = edges[0, 0:1]
+            pairs.append((message.at[row : row + rows], kext.at[base + l]))
+    copies = start(sems, *pairs)
     places[1 : depth + 1] = place[0:depth]
-    places[depth + 1 : depth + 2] = edges[1, 0:1]
-
-    @pl.when(flat == 0)
-    def _():
-        kext[1] = kext[2]
-
-    @pl.when(flat == last)
-    def _():
-        kext[depth + 2] = kext[depth + 1]
+    finish(copies[:2])
 
     row = iota((rows, cols), 0)
     col = iota((rows, cols), 1)
@@ -337,7 +326,7 @@
         total = total + back * before + front * after
         return jnp.where(row == level, 0.0, total)
 
-    fext[:, :, level : level + 1, :] = jnp.zeros((3, depth + 4, 1, cols), F32)
+    fext[:, 2 : depth + 2, level : level + 1, :] = jnp.zeros((3, depth, 1, cols), F32)
 
     def first_sweep(i, carry):
         l = i + 1
@@ -360,7 +349,23 @@
             mext[comp, i] = blend(w, fext[comp, l], fext[comp, l - 1], fext[comp, l + 1]) * keep
         return carry
 
-    lax.fori_loop(0, depth + 2, first_sweep, 0)
+    lax.fori_loop(2, depth, first_sweep, 0)
+    finish(copies[2:])
+    places[0:1] = edges[0, 0:1]
+    places[depth + 1 : depth + 2] = edges[1, 0:1]
+    fext[:, 0:2, level : level + 1, :] = jnp.zeros((3, 2, 1, cols), F32)
+    fext[:, depth + 2 : depth + 4, level : level + 1, :] = jnp.zeros((3, 2, 1, cols), F32)
+
+    @pl.when(flat == 0)
+    def _():
+        kext[1] = kext[2]
+
+    @pl.when(flat == last)
+    def _():
+        kext[depth + 2] = kext[depth + 1]
+
+    lax.fori_loop(0, 2, first_sweep, 0)
+    lax.fori_loop(depth, depth + 2, first_sweep, 0)
 
     def second_sweep(z):
         w = weights(z + 2)
@@ -513,9 +518,10 @@
     )
     root = groups - 1
     none = jnp.zeros((8, EXT), F32)
-    others = [lax.ppermute(mine, "grp", [(g, root)]) for g in range(root)] + [none] * (4 - groups)
-    low_rows = lax.ppermute(low_end, "grp", [(g, g + 1) for g in range(root)])
-    high_rows = lax.ppermute(high_end, "grp", [(g + 1, g) for g in range(root)])
+    others = []
+    for g in range(root):
+        others.append(lax.ppermute(mine, "grp", [(g, root)]))
+    others += [none] * (4 - groups)
     load, first, partial, spill, edge = call(
         load_kernel,
         [mine, *others, diag, ghost, conn, held, table],
@@ -534,18 +540,13 @@
         mib=16,
         name="step_vvvvvvvvvv_vv",
     )
-    others = [lax.ppermute(second, "grp", [(root, g)]) for g in range(root)] + [none] * (4 - groups)
-    (send,) = call(
-        reply_kernel,
-        [second, *others, kept, low_rows, high_rows],
-        [shape(6 * slabs, 128)],
-        [],
-        mib=12,
-        name="reply_vvvvvvv_v",
-    )
-    back = exchange(send, 6, slabs)
+    others = []
+    for g in range(root):
+        others.append(lax.ppermute(second, "grp", [(root, g)]))
+    others += [none] * (4 - groups)
     spill_low = lax.ppermute(spill, AXES, shell_up)
-    shell_disp = second[:6, :NODES].at[:, :NB].add(-(precond[:, :NB] * spill_low[:6]))
+    low_rows = lax.ppermute(low_end, "grp", [(g, g + 1) for g in range(root)])
+    high_rows = lax.ppermute(high_end, "grp", [(g + 1, g) for g in range(root)])
     base, mid = call(
         sweep_kernel,
         [mesh_disp, kappa, place, low, high],
@@ -563,6 +564,15 @@
         mib=16,
         name="sweep_hhvaa_hv",
     )
+    send, shell_disp = call(
+        reply_kernel,
+        [second, *others, kept, low_rows, high_rows, diag, spill_low, mid],
+        [shape(6 * slabs, 128), shape(6, NODES)],
+        [],
+        mib=12,
+        name="reply_vvvvvvvvva_vv",
+    )
+    back = exchange(send, 6, slabs)
     (field,) = call(
         lambda *refs: finish_kernel(slabs, *refs),
         [back, mid, base],

time: 93.6 us -> 98.3 us (1.050)
  the two profiles are of different devices: /device:TPU:1 before, /device:TPU:25 now
where the time goes in v4:
time: 98.3 us; the launch traced here: 97.8 us
  starting transfers between devices  41.8 us (43%)
  blocking collectives  22 us (22%)
  Pallas kernels  19.2 us (20%)
  waiting for transfers between devices  12.2 us (12%)
  local copies, waits for them, and re-layouts  1.68 us (2%)
    all_to_all x1, blocking collectives, exchange(): lax.all_to_all(flat, 'slab', 0, 0, tiled=True).reshape(count * per, 128)  22 us
    pallas_call x8, Pallas kernels, call(): pl.pallas_call(kernel, out_shape=outs, in_specs=[kinds[k] for k in into],...  19.2 us
    all_to_all x1, starting transfers between devices, exchange(): lax.all_to_all(flat, 'slab', 0, 0, tiled=True).reshape(count * per, 128)  13 us
    all_to_all x1, waiting for transfers between devices, exchange(): lax.all_to_all(flat, 'slab', 0, 0, tiled=True).reshape(count * per, 128)  7.71 us
    ppermute x2, starting transfers between devices, on_device(): spill_low = lax.ppermute(spill, AXES, shell_up)  7.49 us
    ppermute x3, starting transfers between devices, on_device(): others.append(lax.ppermute(second, 'grp', [(root, g)]))  4.93 us
    ppermute x3, starting transfers between devices, on_device(): others.append(lax.ppermute(mine, 'grp', [(g, root)]))  3.88 us
    ppermute x1, starting transfers between devices, on_device(): low = lax.ppermute(to_up, AXES, up)  3.68 us
  transfers between devices with their start and end apart: 15, of which 4 were waited for; matrix products, arithmetic and copies ran while one was open for 0% of the time, Pallas kernels for 13%

profile of v4, /device:TPU:25, one launch (start us, length us, event | category | flops | bytes accessed | tf_op | source)
XLA Modules:
  0.0 97.8 jit_solution(13705599834725019569)
XLA Ops:
  0.7 3.8 %shard_map.104 = (f32[128,128]{1,0:T(8,128)}, f32[8,256]{1,0:T(8,128)}, f32[1032,256]{1,0:T(8,128)}, f32[1032,256]{1,0:T(8,128)}) custom-call(f32[2,4,256]{2,1,0:T(4,128)} %refs_0_.1, f32[3,4,256]{2,1,0:T(4,128)} %refs_1_.1, s32[8,128]{1,0:T(8,128)} %bitcast.10, s32[8,128]{1,0:T(8,128)} %bitcast.11, f32[3,4,128,256]{3,2,1,0:T(8,128)} %field.1, ...), custom_call_target="tpu_custom_call" | custom-call | tf_op jit(solution)/shard_map/pallas_call | solution.py:445
  4.5 3.7 %collective-permute-start.12 = (f32[1032,256]{1,0:T(8,128)}, f32[1032,256]{1,0:T(8,128)S(1)}, u32[]{:S(2)}, u32[]{:S(2)}) collective-permute-start(f32[1032,256]{1,0:T(8,128)} %get-tuple-element.42), channel_id=1, source_target_pairs={{0,1},{1,2},{2,3},{3,4},{4,5},{5,6},{6,7},{7,8},{8,9},{9,10},{10,1... | collective-permute-start | bytes 3170312 | tf_op jit(solution)/shard_map/ppermute | solution.py:496
  8.1 1.9 %collective-permute-start.13 = (f32[1032,256]{1,0:T(8,128)}, f32[1032,256]{1,0:T(8,128)S(1)}, u32[]{:S(2)}, u32[]{:S(2)}) collective-permute-start(f32[1032,256]{1,0:T(8,128)} %get-tuple-element.43), channel_id=1, source_target_pairs={{1,0},{2,1},{3,2},{4,3},{5,4},{6,5},{7,6},{8,7},{9,8},{10,9},{11,1... | collective-permute-start | bytes 3170312 | tf_op jit(solution)/shard_map/ppermute | solution.py:497
  10.1 13.0 %all-to-all-start = ((f32[64,1,256]{2,1,0:T(1,128)}), f32[64,1,256]{2,1,0:T(1,128)S(1)}, u32[]{:S(2)}, u32[]{:S(2)}) async-start(f32[64,1,256]{2,1,0:T(1,128)} %bitcast.9), calls=%async_computation | async-start | bytes 131072 | tf_op jit(solution)/shard_map/all_to_all | solution.py:458
  23.1 2.4 %collective-permute-start.3 = (f32[6,1024]{1,0:T(8,128)S(1)}, f32[6,1024]{1,0:T(8,128)S(1)}, u32[]{:S(2)}, u32[]{:S(2)}) collective-permute-start(f32[6,1024]{1,0:T(8,128)S(1)} %copy-done.3), channel_id=1, source_target_pairs={{193,192},{194,193},{195,194},{196,195},{197,196},{198,197},{199,1... | collective-permute-start | bytes 73736 | tf_op jit(solution)/shard_map/ppermute | solution.py:475
  25.4 7.7 %all-to-all-done = f32[64,1,256]{2,1,0:T(1,128)S(1)} async-done(((f32[64,1,256]{2,1,0:T(1,128)}), f32[64,1,256]{2,1,0:T(1,128)S(1)}, u32[]{:S(2)}, u32[]{:S(2)}) %all-to-all-start) | async-done | bytes 65568 | tf_op jit(solution)/shard_map/all_to_all | solution.py:458
  33.2 0.9 shard_map.105
  34.0 1.3 %collective-permute-start.2 = (f32[8,1152]{1,0:T(8,128)S(1)}, f32[8,1152]{1,0:T(8,128)S(1)}, u32[]{:S(2)}, u32[]{:S(2)}) collective-permute-start(f32[8,1152]{1,0:T(8,128)S(1)} %get-tuple-element.26.mine), channel_id=1, source_target_pairs={{128,192},{129,193},{130,194},{131,195},{132,196},{133,197},{134,1... | collective-permute-start | bytes 110600 | tf_op jit(solution)/shard_map/ppermute | solution.py:523
  35.3 1.3 %collective-permute-start.1 = (f32[8,1152]{1,0:T(8,128)S(1)}, f32[8,1152]{1,0:T(8,128)S(1)}, u32[]{:S(2)}, u32[]{:S(2)}) collective-permute-start(f32[8,1152]{1,0:T(8,128)S(1)} %get-tuple-element.26.mine), channel_id=1, source_target_pairs={{64,192},{65,193},{66,194},{67,195},{68,196},{69,197},{70,198},{71... | collective-permute-start | bytes 110600 | tf_op jit(solution)/shard_map/ppermute | solution.py:523
  36.6 0.0 collective-permute-done.3.ghost
  36.6 1.3 %collective-permute-start = (f32[8,1152]{1,0:T(8,128)S(1)}, f32[8,1152]{1,0:T(8,128)S(1)}, u32[]{:S(2)}, u32[]{:S(2)}) collective-permute-start(f32[8,1152]{1,0:T(8,128)S(1)} %get-tuple-element.26.mine), channel_id=1, source_target_pairs={{0,192},{1,193},{2,194},{3,195},{4,196},{5,197},{6,198},{7,199},{8... | collective-permute-start | bytes 110600 | tf_op jit(solution)/shard_map/ppermute | solution.py:523
  37.9 0.0 copy-start.1
  37.9 1.7 %copy-done.1 = f32[24,24,1024]{2,1,0:T(8,128)S(1)} copy-done((f32[24,24,1024]{2,1,0:T(8,128)S(1)}, f32[24,24,1024]{2,1,0:T(8,128)}, u32[]{:S(2)}) %copy-start.1) | copy-done | bytes 2359320
  39.6 0.4 shard_map.106
  40.0 1.5 %collective-permute-done.1.other1 = f32[8,1152]{1,0:T(8,128)S(1)} collective-permute-done((f32[8,1152]{1,0:T(8,128)S(1)}, f32[8,1152]{1,0:T(8,128)S(1)}, u32[]{:S(2)}, u32[]{:S(2)}) %collective-permute-start.1) | collective-permute-done | bytes 36896 | tf_op jit(solution)/shard_map/ppermute | solution.py:523
  41.5 1.2 %collective-permute-done.other0 = f32[8,1152]{1,0:T(8,128)S(1)} collective-permute-done((f32[8,1152]{1,0:T(8,128)S(1)}, f32[8,1152]{1,0:T(8,128)S(1)}, u32[]{:S(2)}, u32[]{:S(2)}) %collective-permute-start) | collective-permute-done | bytes 36896 | tf_op jit(solution)/shard_map/ppermute | solution.py:523
  42.8 1.4 %shard_map.107 = (f32[8,1152]{1,0:T(8,128)S(1)}, f32[8,1152]{1,0:T(8,128)S(1)}, f32[8,1152]{1,0:T(8,128)S(1)}, f32[8,128]{1,0:T(8,128)S(1)}, f32[8,128]{1,0:T(8,128)S(1)}) custom-call(f32[8,1152]{1,0:T(8,128)S(1)} %get-tuple-element.26.mine, f32[8,1152]{1,0:T(8,128)S(1)} %collective-permute-done.other0, f32[8,1152]{1,0:T(8,128)S(1)} %collective-permute-done.1.other1, ...), custom_call_target="tpu_custom_call" | custom-call | tf_op jit(solution)/shard_map/pallas_call | solution.py:445
  44.2 3.3 %collective-permute-start.4 = (f32[8,128]{1,0:T(8,128)S(1)}, f32[8,128]{1,0:T(8,128)S(1)}, u32[]{:S(2)}, u32[]{:S(2)}) collective-permute-start(f32[8,128]{1,0:T(8,128)S(1)} %get-tuple-element.34), channel_id=1, source_target_pairs={{192,193},{193,194},{194,195},{195,196},{196,197},{197,198},{198,1... | collective-permute-start | bytes 12296 | tf_op jit(solution)/shard_map/ppermute | solution.py:533
  47.5 1.9 %collective-permute-start.5 = (f32[8,128]{1,0:T(8,128)S(1)}, f32[8,128]{1,0:T(8,128)S(1)}, u32[]{:S(2)}, u32[]{:S(2)}) collective-permute-start(f32[8,128]{1,0:T(8,128)S(1)} %get-tuple-element.35), channel_id=1, source_target_pairs={{193,192},{194,193},{195,194},{196,195},{197,196},{198,197},{199,1... | collective-permute-start | bytes 12296 | tf_op jit(solution)/shard_map/ppermute | solution.py:534
  49.4 1.3 %collective-permute-start.9 = (f32[8,128]{1,0:T(8,128)S(1)}, f32[8,128]{1,0:T(8,128)S(1)}, u32[]{:S(2)}, u32[]{:S(2)}) collective-permute-start(f32[8,128]{1,0:T(8,128)S(1)} %get-tuple-element.38), channel_id=1, source_target_pairs={{0,64},{64,128},{128,192},{1,65},{65,129},{129,193},{2,66},{66,130... | collective-permute-start | bytes 12296 | tf_op jit(solution)/shard_map/ppermute | solution.py:548
  50.7 1.7 %collective-permute-done.5.from_high = f32[8,128]{1,0:T(8,128)S(1)} collective-permute-done((f32[8,128]{1,0:T(8,128)S(1)}, f32[8,128]{1,0:T(8,128)S(1)}, u32[]{:S(2)}, u32[]{:S(2)}) %collective-permute-start.5) | collective-permute-done | bytes 4128 | tf_op jit(solution)/shard_map/ppermute | solution.py:534
  52.4 1.4 %shard_map.108 = (f32[8,1152]{1,0:T(8,128)S(1)}, f32[8,128]{1,0:T(8,128)S(1)}) custom-call(f32[8,1152]{1,0:T(8,128)S(1)} %get-tuple-element.31.load, f32[8,1152]{1,0:T(8,128)S(1)} %get-tuple-element.32.first, f32[8,1152]{1,0:T(8,128)S(1)} %get-tuple-element.33.partial, f32[8,128]{1,0:T(8,128)S(1)} %collective-permute-done.4.from_low, ...), custom_call_target="tpu_custom_call" | custom-call | tf_op jit(solution)/shard_map/pallas_call | solution.py:445
  53.8 2.3 %collective-permute-start.8 = (f32[8,1152]{1,0:T(8,128)S(1)}, f32[8,1152]{1,0:T(8,128)S(1)}, u32[]{:S(2)}, u32[]{:S(2)}) collective-permute-start(f32[8,1152]{1,0:T(8,128)S(1)} %get-tuple-element.36.mine), channel_id=1, source_target_pairs={{192,128},{193,129},{194,130},{195,131},{196,132},{197,133},{198,1... | collective-permute-start | bytes 110600 | tf_op jit(solution)/shard_map/ppermute | solution.py:545
  56.2 1.3 %collective-permute-start.7 = (f32[8,1152]{1,0:T(8,128)S(1)}, f32[8,1152]{1,0:T(8,128)S(1)}, u32[]{:S(2)}, u32[]{:S(2)}) collective-permute-start(f32[8,1152]{1,0:T(8,128)S(1)} %get-tuple-element.36.mine), channel_id=1, source_target_pairs={{192,64},{193,65},{194,66},{195,67},{196,68},{197,69},{198,70},{19... | collective-permute-start | bytes 110600 | tf_op jit(solution)/shard_map/ppermute | solution.py:545
  57.5 1.3 %collective-permute-start.6 = (f32[8,1152]{1,0:T(8,128)S(1)}, f32[8,1152]{1,0:T(8,128)S(1)}, u32[]{:S(2)}, u32[]{:S(2)}) collective-permute-start(f32[8,1152]{1,0:T(8,128)S(1)} %get-tuple-element.36.mine), channel_id=1, source_target_pairs={{192,0},{193,1},{194,2},{195,3},{196,4},{197,5},{198,6},{199,7},{2... | collective-permute-start | bytes 110600 | tf_op jit(solution)/shard_map/ppermute | solution.py:545
  58.8 1.3 %collective-permute-start.10 = (f32[8,128]{1,0:T(8,128)S(1)}, f32[8,128]{1,0:T(8,128)S(1)}, u32[]{:S(2)}, u32[]{:S(2)}) collective-permute-start(f32[8,128]{1,0:T(8,128)S(1)} %get-tuple-element.39), channel_id=1, source_target_pairs={{64,0},{128,64},{192,128},{65,1},{129,65},{193,129},{66,2},{130,66... | collective-permute-start | bytes 12296 | tf_op jit(solution)/shard_map/ppermute | solution.py:549
  60.1 4.2 %collective-permute-start.11 = (f32[8,128]{1,0:T(8,128)S(1)}, f32[8,128]{1,0:T(8,128)S(1)}, u32[]{:S(2)}, u32[]{:S(2)}) collective-permute-start(f32[8,128]{1,0:T(8,128)S(1)} %get-tuple-element.40), channel_id=1, source_target_pairs={{192,193},{193,194},{194,195},{195,196},{196,197},{197,198},{198,1... | collective-permute-start | bytes 12296 | tf_op jit(solution)/shard_map/ppermute | solution.py:547
  64.4 8.8 %shard_map.109 = (f32[3,4,128,256]{3,2,1,0:T(8,128)}, f32[18,16,256]{2,1,0:T(8,128)S(1)}) custom-call(f32[3,4,128,256]{3,2,1,0:T(8,128)S(1)} %copy-done, f32[4,128,256]{2,1,0:T(8,128)S(1)} %copy-done.2, f32[8,256]{1,0:T(8,128)S(1)} %copy-done.5, f32[1032,256]{1,0:T(8,128)S(1)} %collective-permute-done.12.low, f32[1032,256]{1,0:T(8,128)S(1)} %collective-permute-done.13.high), custom_call_target="tpu_custom_call" | custom-call | tf_op jit(solution)/shard_map/pallas_call | solution.py:445
  73.1 0.0 collective-permute-done.11.from_low
  73.2 1.5 %shard_map.110 = (f32[384,128]{1,0:T(8,128)S(1)}, f32[6,1024]{1,0:T(8,128)}) custom-call(f32[8,1152]{1,0:T(8,128)S(1)} %get-tuple-element.36.mine, f32[8,1152]{1,0:T(8,128)S(1)} %collective-permute-done.6.other0, f32[8,1152]{1,0:T(8,128)S(1)} %collective-permute-done.7.other1, f32[8,1152]{1,0:T(8,128)S(1)} %collective-permute-done.8.other2, ...), custom_call_target="tpu_custom_call" | custom-call | tf_op jit(solution)/shard_map/pallas_call | solution.py:445
  74.6 22.0 %all_to_all.10 = f32[64,1,768]{2,1,0:T(1,128)S(1)} all-to-all(f32[64,1,768]{2,1,0:T(1,128)S(1)} %bitcast.8), channel_id=1, replica_groups=mesh['grp'=4,'slab'=64] {'slab'}, dimensions={0} | all-to-all | bytes 393216 | tf_op jit(solution)/shard_map/all_to_all | solution.py:458
  96.7 1.1 %shard_map.111 = f32[3,4,128,256]{3,2,1,0:T(8,128)} custom-call(f32[384,128]{1,0:T(8,128)S(1)} %bitcast.6, f32[18,16,256]{2,1,0:T(8,128)S(1)} %get-tuple-element.44.swept.refs_1_, f32[3,4,128,256]{3,2,1,0:T(8,128)} %get-tuple-element.46.refs_2_), custom_call_target="tpu_custom_call", output_to_operand_aliasing={{}: (2, {})} | custom-call | tf_op jit(solution)/shard_map/pallas_call | solution.py:445
  (19 shorter events, 0.0 us)
Async XLA Ops:
  0.6 22.4 %copy-start.3 = (f32[6,1024]{1,0:T(8,128)S(1)}, f32[6,1024]{1,0:T(8,128)}, u32[]{:S(2)}) copy-start(f32[6,1024]{1,0:T(8,128)} %precond_in.1) | copy-start | bytes 73732
  0.6 37.3 %copy-start.4 = (s32[4,1024]{1,0:T(4,128)S(1)}, s32[4,1024]{1,0:T(4,128)}, u32[]{:S(2)}) copy-start(s32[4,1024]{1,0:T(4,128)} %conn_in.1) | copy-start | bytes 49156
  4.5 54.4 %collective-permute-start.12 = (f32[1032,256]{1,0:T(8,128)}, f32[1032,256]{1,0:T(8,128)S(1)}, u32[]{:S(2)}, u32[]{:S(2)}) collective-permute-start(f32[1032,256]{1,0:T(8,128)} %get-tuple-element.42), channel_id=1, source_target_pairs={{0,1},{1,2},{2,3},{3,4},{4,5},{5,6},{6,7},{7,8},{8,9},{9,10},{10,1... | collective-permute-start | bytes 3170312 | tf_op jit(solution)/shard_map/ppermute | solution.py:496
  8.1 52.0 %collective-permute-start.13 = (f32[1032,256]{1,0:T(8,128)}, f32[1032,256]{1,0:T(8,128)S(1)}, u32[]{:S(2)}, u32[]{:S(2)}) collective-permute-start(f32[1032,256]{1,0:T(8,128)} %get-tuple-element.43), channel_id=1, source_target_pairs={{1,0},{2,1},{3,2},{4,3},{5,4},{6,5},{7,6},{8,7},{9,8},{10,9},{11,1... | collective-permute-start | bytes 3170312 | tf_op jit(solution)/shard_map/ppermute | solution.py:497
  10.1 23.1 %all-to-all-start = ((f32[64,1,256]{2,1,0:T(1,128)}), f32[64,1,256]{2,1,0:T(1,128)S(1)}, u32[]{:S(2)}, u32[]{:S(2)}) async-start(f32[64,1,256]{2,1,0:T(1,128)} %bitcast.9), calls=%async_computation | async-start | bytes 131072 | tf_op jit(solution)/shard_map/all_to_all | solution.py:458
  23.1 13.5 %collective-permute-start.3 = (f32[6,1024]{1,0:T(8,128)S(1)}, f32[6,1024]{1,0:T(8,128)S(1)}, u32[]{:S(2)}, u32[]{:S(2)}) collective-permute-start(f32[6,1024]{1,0:T(8,128)S(1)} %copy-done.3), channel_id=1, source_target_pairs={{193,192},{194,193},{195,194},{196,195},{197,196},{198,197},{199,1... | collective-permute-start | bytes 73736 | tf_op jit(solution)/shard_map/ppermute | solution.py:475
  34.0 6.0 %collective-permute-start.2 = (f32[8,1152]{1,0:T(8,128)S(1)}, f32[8,1152]{1,0:T(8,128)S(1)}, u32[]{:S(2)}, u32[]{:S(2)}) collective-permute-start(f32[8,1152]{1,0:T(8,128)S(1)} %get-tuple-element.26.mine), channel_id=1, source_target_pairs={{128,192},{129,193},{130,194},{131,195},{132,196},{133,197},{134,1... | collective-permute-start | bytes 110600 | tf_op jit(solution)/shard_map/ppermute | solution.py:523
  35.3 6.2 %collective-permute-start.1 = (f32[8,1152]{1,0:T(8,128)S(1)}, f32[8,1152]{1,0:T(8,128)S(1)}, u32[]{:S(2)}, u32[]{:S(2)}) collective-permute-start(f32[8,1152]{1,0:T(8,128)S(1)} %get-tuple-element.26.mine), channel_id=1, source_target_pairs={{64,192},{65,193},{66,194},{67,195},{68,196},{69,197},{70,198},{71... | collective-permute-start | bytes 110600 | tf_op jit(solution)/shard_map/ppermute | solution.py:523
  36.6 6.1 %collective-permute-start = (f32[8,1152]{1,0:T(8,128)S(1)}, f32[8,1152]{1,0:T(8,128)S(1)}, u32[]{:S(2)}, u32[]{:S(2)}) collective-permute-start(f32[8,1152]{1,0:T(8,128)S(1)} %get-tuple-element.26.mine), channel_id=1, source_target_pairs={{0,192},{1,193},{2,194},{3,195},{4,196},{5,197},{6,198},{7,199},{8... | collective-permute-start | bytes 110600 | tf_op jit(solution)/shard_map/ppermute | solution.py:523
  37.9 1.7 %copy-start.1 = (f32[24,24,1024]{2,1,0:T(8,128)S(1)}, f32[24,24,1024]{2,1,0:T(8,128)}, u32[]{:S(2)}) copy-start(f32[24,24,1024]{2,1,0:T(8,128)} %stiffness.1) | copy-start | bytes 7077892
  44.2 6.5 %collective-permute-start.4 = (f32[8,128]{1,0:T(8,128)S(1)}, f32[8,128]{1,0:T(8,128)S(1)}, u32[]{:S(2)}, u32[]{:S(2)}) collective-permute-start(f32[8,128]{1,0:T(8,128)S(1)} %get-tuple-element.34), channel_id=1, source_target_pairs={{192,193},{193,194},{194,195},{195,196},{196,197},{197,198},{198,1... | collective-permute-start | bytes 12296 | tf_op jit(solution)/shard_map/ppermute | solution.py:533
  47.5 4.9 %collective-permute-start.5 = (f32[8,128]{1,0:T(8,128)S(1)}, f32[8,128]{1,0:T(8,128)S(1)}, u32[]{:S(2)}, u32[]{:S(2)}) collective-permute-start(f32[8,128]{1,0:T(8,128)S(1)} %get-tuple-element.35), channel_id=1, source_target_pairs={{193,192},{194,193},{195,194},{196,195},{197,196},{198,197},{199,1... | collective-permute-start | bytes 12296 | tf_op jit(solution)/shard_map/ppermute | solution.py:534
  49.4 8.1 %collective-permute-start.9 = (f32[8,128]{1,0:T(8,128)S(1)}, f32[8,128]{1,0:T(8,128)S(1)}, u32[]{:S(2)}, u32[]{:S(2)}) collective-permute-start(f32[8,128]{1,0:T(8,128)S(1)} %get-tuple-element.38), channel_id=1, source_target_pairs={{0,64},{64,128},{128,192},{1,65},{65,129},{129,193},{2,66},{66,130... | collective-permute-start | bytes 12296 | tf_op jit(solution)/shard_map/ppermute | solution.py:548
  52.4 11.9 %copy-start = (f32[3,4,128,256]{3,2,1,0:T(8,128)S(1)}, f32[3,4,128,256]{3,2,1,0:T(8,128)}, u32[]{:S(2)}) copy-start(f32[3,4,128,256]{3,2,1,0:T(8,128)} %field.1) | copy-start | bytes 4718596
  52.4 11.9 %copy-start.2 = (f32[4,128,256]{2,1,0:T(8,128)S(1)}, f32[4,128,256]{2,1,0:T(8,128)}, u32[]{:S(2)}) copy-start(f32[4,128,256]{2,1,0:T(8,128)} %kappa.1) | copy-start | bytes 1572868
  52.4 11.9 %copy-start.5 = (f32[8,256]{1,0:T(8,128)S(1)}, f32[8,256]{1,0:T(8,128)}, u32[]{:S(2)}) copy-start(f32[8,256]{1,0:T(8,128)} %get-tuple-element.41.place) | copy-start | bytes 24580
  53.8 19.3 %collective-permute-start.8 = (f32[8,1152]{1,0:T(8,128)S(1)}, f32[8,1152]{1,0:T(8,128)S(1)}, u32[]{:S(2)}, u32[]{:S(2)}) collective-permute-start(f32[8,1152]{1,0:T(8,128)S(1)} %get-tuple-element.36.mine), channel_id=1, source_target_pairs={{192,128},{193,129},{194,130},{195,131},{196,132},{197,133},{198,1... | collective-permute-start | bytes 110600 | tf_op jit(solution)/shard_map/ppermute | solution.py:545
  56.2 17.0 %collective-permute-start.7 = (f32[8,1152]{1,0:T(8,128)S(1)}, f32[8,1152]{1,0:T(8,128)S(1)}, u32[]{:S(2)}, u32[]{:S(2)}) collective-permute-start(f32[8,1152]{1,0:T(8,128)S(1)} %get-tuple-element.36.mine), channel_id=1, source_target_pairs={{192,64},{193,65},{194,66},{195,67},{196,68},{197,69},{198,70},{19... | collective-permute-start | bytes 110600 | tf_op jit(solution)/shard_map/ppermute | solution.py:545
  57.5 15.7 %collective-permute-start.6 = (f32[8,1152]{1,0:T(8,128)S(1)}, f32[8,1152]{1,0:T(8,128)S(1)}, u32[]{:S(2)}, u32[]{:S(2)}) collective-permute-start(f32[8,1152]{1,0:T(8,128)S(1)} %get-tuple-element.36.mine), channel_id=1, source_target_pairs={{192,0},{193,1},{194,2},{195,3},{196,4},{197,5},{198,6},{199,7},{2... | collective-permute-start | bytes 110600 | tf_op jit(solution)/shard_map/ppermute | solution.py:545
  58.8 14.3 %collective-permute-start.10 = (f32[8,128]{1,0:T(8,128)S(1)}, f32[8,128]{1,0:T(8,128)S(1)}, u32[]{:S(2)}, u32[]{:S(2)}) collective-permute-start(f32[8,128]{1,0:T(8,128)S(1)} %get-tuple-element.39), channel_id=1, source_target_pairs={{64,0},{128,64},{192,128},{65,1},{129,65},{193,129},{66,2},{130,66... | collective-permute-start | bytes 12296 | tf_op jit(solution)/shard_map/ppermute | solution.py:549
  60.1 13.0 %collective-permute-start.11 = (f32[8,128]{1,0:T(8,128)S(1)}, f32[8,128]{1,0:T(8,128)S(1)}, u32[]{:S(2)}, u32[]{:S(2)}) collective-permute-start(f32[8,128]{1,0:T(8,128)S(1)} %get-tuple-element.40), channel_id=1, source_target_pairs={{192,193},{193,194},{194,195},{195,196},{196,197},{197,198},{198,1... | collective-permute-start | bytes 12296 | tf_op jit(solution)/shard_map/ppermute | solution.py:547
